TPU v7x, 32 devices: a whole 2x2x4 slice. The times are simulated.
32 devices in a mesh: fsdp: 4 (over z), ctx: 4 (over y, x), tp: 2 (over core).
Axes of the slice: x: 2, y: 2, z: 4, core: 2. Of those that a mesh axis runs over, the one named last changes fastest.
Arguments:
- layer_input: bfloat16 [2048, 8, 768], P('ctx', 'fsdp'), may hold values from -6 to 6
- output_cotangent: bfloat16 [2048, 8, 768], P('ctx', 'fsdp'), may hold values from -6 to 6
- prefix_len: int32 [8], P('fsdp'), may hold values from 204 to 1024, as said below
- attn_gain: float32 [768], P('fsdp'), may hold values from 0.25 to 1.75
- mlp_gain: float32 [768], P('fsdp'), may hold values from 0.25 to 1.75
- query_weight: float32 [768, 768], P('fsdp', 'tp'), may hold values from -0.21875 to 0.21875
- key_weight: float32 [768, 768], P('fsdp', 'tp'), may hold values from -0.21875 to 0.21875
- value_weight: float32 [768, 768], P('fsdp', 'tp'), may hold values from -0.21875 to 0.21875
- out_weight: float32 [768, 768], P('tp', 'fsdp'), may hold values from -4.8 to 4.8
- gate_weight: float32 [768, 2048], P('fsdp', 'tp'), may hold values from -0.21875 to 0.21875
- up_weight: float32 [768, 2048], P('fsdp', 'tp'), may hold values from -0.21875 to 0.21875
- down_weight: float32 [2048, 768], P('tp', 'fsdp'), may hold values from -0.125 to 0.125
Outputs:
- layer_output: bfloat16 [2048, 8, 768], P('ctx', 'fsdp')
- input_grad: bfloat16 [2048, 8, 768], P('ctx', 'fsdp')
- attn_gain_grad: float32 [768], P('fsdp')
- mlp_gain_grad: float32 [768], P('fsdp')
- query_weight_grad: float32 [768, 768], P('fsdp', 'tp')
- key_weight_grad: float32 [768, 768], P('fsdp', 'tp')
- value_weight_grad: float32 [768, 768], P('fsdp', 'tp')
- out_weight_grad: float32 [768, 768], P('tp', 'fsdp')
- gate_weight_grad: float32 [768, 2048], P('fsdp', 'tp')
- up_weight_grad: float32 [768, 2048], P('fsdp', 'tp')
- down_weight_grad: float32 [2048, 768], P('tp', 'fsdp')
Inputs may be any that keep to these rules, and one draw needn't show every extreme that they name: `prefix_len`: number of leading positions of each sequence that all its queries see; one sequence has each bound.
All inputs are finite; a program needn't handle non-finite values.
Results may differ from a plain program's by a relative error of at most 0.025.
Values may be sent and summed in bfloat16 or wider, within the bound.
A program may use at most 128 MiB of HBM per device.

v0:
```python
import math

import jax
import jax.numpy as jnp
from jax import lax
from jax.sharding import PartitionSpec as P

HEAD_DIM = 64


EPS = 1e-06
BASE = 10000.0
MASKED = -1e30


def partner(block, axis, apart):
    count = lax.axis_size(axis)
    route = []
    for low in range(count):
        high = low | 1 << apart
        if high != low and high < count:
            route += [(low, high), (high, low)]
    return lax.ppermute(block, axis, route)


def from_behind(value, axis, steps):
    count = lax.axis_size(axis)
    pairs = [(source, (source + steps) % count) for source in range(count)]
    return lax.ppermute(value, axis, pairs)


def norm_rows(values, gain):
    return values * lax.rsqrt(jnp.mean(values * values, axis=-1, keepdims=True) + EPS) * gain


def rope_tables(positions):
    half_dim = HEAD_DIM // 2
    frequency = jnp.exp(
        jnp.arange(half_dim, dtype=jnp.float32) * (-2.0 * math.log(BASE) / HEAD_DIM)
    )
    angles = positions.astype(jnp.float32)[:, None] * frequency[None, :]
    cos_table = jnp.concatenate([jnp.cos(angles), jnp.cos(angles)], axis=1)
    sine_table = jnp.concatenate([jnp.sin(angles), jnp.sin(angles)], axis=1)
    return (cos_table[:, None, None, :], sine_table[:, None, None, :])


def rotary(values, cos_table, sine_table):
    half_dim = values.shape[-1] // 2
    turned = jnp.concatenate([-values[..., half_dim:], values[..., :half_dim]], axis=-1)
    return values * cos_table + turned * sine_table


def unrotary(grads, cos_table, sine_table):
    half_dim = grads.shape[-1] // 2
    scaled = grads * sine_table
    turned = jnp.concatenate([scaled[..., half_dim:], -scaled[..., :half_dim]], axis=-1)
    return grads * cos_table + turned


def block_positions(device, block_len, ctx_size):
    half_len = block_len // 2
    steps = jnp.arange(half_len, dtype=jnp.int32)
    first_part = 2 * device * half_len + steps
    second_part = (2 * ctx_size - 1 - 2 * device) * half_len + steps
    return jnp.concatenate([first_part, second_part], axis=0)


def mirror_rows(values):
    ctx_bits = lax.axis_size("ctx").bit_length() - 1
    for bit in range(ctx_bits):
        values = partner(values, "ctx", bit)
    return values


def visible(prefix_len, query_pos, key_pos):
    causal = key_pos[None, :] <= query_pos[:, None]
    opened = key_pos[None, None, :] < prefix_len[:, None, None]
    return (causal[None] | opened)[:, None]


def block_needed(prefix_len, query_pos, key_pos):
    first_key = jnp.min(key_pos)
    return (first_key <= jnp.max(query_pos)) | jnp.any(prefix_len > first_key)


def attend_step(softmax_state, queries, key_value, prefix_len, query_pos, key_pos):
    key_heads = key_value[..., :HEAD_DIM]
    value_heads = key_value[..., HEAD_DIM:]

    def compute(state_in):
        row_max, row_sum, weighted = state_in
        scores = jnp.einsum(
            "qshd,kshd->shqk", queries, key_heads, preferred_element_type=jnp.float32
        ) * HEAD_DIM ** (-0.5)
        allowed = visible(prefix_len, query_pos, key_pos)
        block_max = jnp.max(jnp.where(allowed, scores, MASKED), axis=-1)
        fresh_max = jnp.maximum(row_max, block_max)
        exps = jnp.where(allowed, jnp.exp(scores - fresh_max[..., None]), 0.0)
        factor = jnp.exp(row_max - fresh_max)
        row_sum = row_sum * factor + jnp.sum(exps, axis=-1)
        weighted = weighted * jnp.transpose(factor, (2, 0, 1))[..., None] + jnp.einsum(
            "shqk,kshd->qshd",
            exps.astype(jnp.bfloat16),
            value_heads,
            preferred_element_type=jnp.float32,
        )
        return (fresh_max, row_sum, weighted)

    def skipped(state_in):
        return state_in

    return lax.cond(block_needed(prefix_len, query_pos, key_pos), compute, skipped, softmax_state)


def attend_back(
    queries, attn_grad, log_total, delta_rows, key_value, prefix_len, query_pos, key_pos
):
    key_heads = key_value[..., :HEAD_DIM]
    value_heads = key_value[..., HEAD_DIM:]
    score_scale = HEAD_DIM ** (-0.5)

    def compute(unused):
        scores = (
            jnp.einsum("qshd,kshd->shqk", queries, key_heads, preferred_element_type=jnp.float32)
            * score_scale
        )
        allowed = visible(prefix_len, query_pos, key_pos)
        probabilities = jnp.where(allowed, jnp.exp(scores - log_total[..., None]), 0.0)
        prob_grad = jnp.einsum(
            "qshd,kshd->shqk", attn_grad, value_heads, preferred_element_type=jnp.float32
        )
        score_grad = (probabilities * (prob_grad - delta_rows[..., None])).astype(jnp.bfloat16)
        query_part = (
            jnp.einsum("shqk,kshd->qshd", score_grad, key_heads, preferred_element_type=jnp.float32)
            * score_scale
        )
        key_part = (
            jnp.einsum("shqk,qshd->kshd", score_grad, queries, preferred_element_type=jnp.float32)
            * score_scale
        )
        value_part = jnp.einsum(
            "shqk,qshd->kshd",
            probabilities.astype(jnp.bfloat16),
            attn_grad,
            preferred_element_type=jnp.float32,
        )
        return (query_part, jnp.concatenate([key_part, value_part], axis=-1))

    def skipped(unused):
        return (jnp.zeros(queries.shape, jnp.float32), jnp.zeros(key_value.shape, jnp.float32))

    return lax.cond(block_needed(prefix_len, query_pos, key_pos), compute, skipped, 0)


def pass_grads(key_grads):
    return from_behind(key_grads.astype(jnp.bfloat16), "ctx", 1).astype(key_grads.dtype)


def body(
    layer_input,
    output_cotangent,
    prefix_len,
    attn_gain,
    mlp_gain,
    query_weight,
    key_weight,
    value_weight,
    out_weight,
    gate_weight,
    up_weight,
    down_weight,
):
    block_len, seq_count, width = layer_input.shape
    half_len = block_len // 2
    ctx_size = lax.axis_size("ctx")
    ctx_index = lax.axis_index("ctx")
    moved = mirror_rows(jnp.stack([layer_input[half_len:], output_cotangent[half_len:]], axis=0))
    layer_input = jnp.concatenate([layer_input[:half_len], moved[0]], axis=0)
    output_cotangent = jnp.concatenate([output_cotangent[:half_len], moved[1]], axis=0)
    query_pos = block_positions(ctx_index, block_len, ctx_size)
    cos_table, sine_table = rope_tables(query_pos)
    gain_one, full_query, full_key, full_value, full_out = (
        lax.all_gather(attn_gain.astype(jnp.bfloat16), "fsdp", axis=0, tiled=True),
        lax.all_gather(query_weight.astype(jnp.bfloat16), "fsdp", axis=0, tiled=True),
        lax.all_gather(key_weight.astype(jnp.bfloat16), "fsdp", axis=0, tiled=True),
        lax.all_gather(value_weight.astype(jnp.bfloat16), "fsdp", axis=0, tiled=True),
        lax.all_gather(out_weight.astype(jnp.bfloat16), "fsdp", axis=1, tiled=True),
    )
    gain_two, full_gate, full_up, full_down = (
        lax.all_gather(mlp_gain.astype(jnp.bfloat16), "fsdp", axis=0, tiled=True),
        lax.all_gather(gate_weight.astype(jnp.bfloat16), "fsdp", axis=0, tiled=True),
        lax.all_gather(up_weight.astype(jnp.bfloat16), "fsdp", axis=0, tiled=True),
        lax.all_gather(down_weight.astype(jnp.bfloat16), "fsdp", axis=1, tiled=True),
    )
    heads_local = full_query.shape[1] // HEAD_DIM
    inputs = layer_input.astype(jnp.float32)
    attn_scale = gain_one.astype(jnp.float32)
    normed_low = norm_rows(inputs, attn_scale).astype(jnp.bfloat16)

    def project(matrix):
        product = jnp.einsum("bsd,de->bse", normed_low, matrix, preferred_element_type=jnp.float32)
        return product.reshape(block_len, seq_count, heads_local, HEAD_DIM)

    queries = rotary(project(full_query), cos_table, sine_table).astype(jnp.bfloat16)
    key_heads = rotary(project(full_key), cos_table, sine_table).astype(jnp.bfloat16)
    value_heads = project(full_value).astype(jnp.bfloat16)
    key_value = jnp.concatenate([key_heads, value_heads], axis=-1)
    stats_shape = (seq_count, heads_local, block_len)
    initial = (
        jnp.full(stats_shape, MASKED, jnp.float32),
        jnp.zeros(stats_shape, jnp.float32),
        jnp.zeros((block_len, seq_count, heads_local, HEAD_DIM), jnp.float32),
    )
    softmax_state = attend_step(initial, queries, key_value, prefix_len, query_pos, query_pos)

    def forward_shift(counter, loop_carry):
        state_in, moving = loop_carry
        moving = from_behind(moving, "ctx", 1)
        source = (ctx_index - counter) % ctx_size
        key_pos = block_positions(source, block_len, ctx_size)
        state_in = attend_step(state_in, queries, moving, prefix_len, query_pos, key_pos)
        return (state_in, moving)

    softmax_state, unused_keys = lax.fori_loop(
        1, ctx_size, forward_shift, (softmax_state, key_value)
    )
    row_max, row_sum, weighted = softmax_state
    log_total = row_max + jnp.log(row_sum)
    attn_exact = weighted / jnp.transpose(row_sum, (2, 0, 1))[..., None]
    mixed_low = attn_exact.reshape(block_len, seq_count, heads_local * HEAD_DIM).astype(
        jnp.bfloat16
    )
    attn_part = jnp.einsum("bse,ed->bsd", mixed_low, full_out, preferred_element_type=jnp.float32)
    hidden = inputs + lax.psum(attn_part.astype(jnp.bfloat16), "tp").astype(jnp.float32)
    mlp_scale = gain_two.astype(jnp.float32)
    hnorm_low = norm_rows(hidden, mlp_scale).astype(jnp.bfloat16)
    gate_out = jnp.einsum("bsd,df->bsf", hnorm_low, full_gate, preferred_element_type=jnp.float32)
    up_out = jnp.einsum("bsd,df->bsf", hnorm_low, full_up, preferred_element_type=jnp.float32)
    activated = (jax.nn.silu(gate_out) * up_out).astype(jnp.bfloat16)
    down_part = jnp.einsum("bsf,fd->bsd", activated, full_down, preferred_element_type=jnp.float32)
    result = hidden + lax.psum(down_part.astype(jnp.bfloat16), "tp").astype(jnp.float32)
    layer_output = result.astype(jnp.bfloat16)
    grad_float = output_cotangent.astype(jnp.float32)
    down_w_grad = jnp.einsum(
        "bsf,bsd->fd", activated, output_cotangent, preferred_element_type=jnp.float32
    )
    act_grad = jnp.einsum(
        "bsd,fd->bsf", output_cotangent, full_down, preferred_element_type=jnp.float32
    )
    unused_value, silu_pullback = jax.vjp(
        lambda gate_in, up_in: jax.nn.silu(gate_in) * up_in, gate_out, up_out
    )
    gate_back, up_back = silu_pullback(act_grad)
    gate_grad = gate_back.astype(jnp.bfloat16)
    up_grad = up_back.astype(jnp.bfloat16)
    gate_w_grad = jnp.einsum(
        "bsd,bsf->df", hnorm_low, gate_grad, preferred_element_type=jnp.float32
    )
    up_w_grad = jnp.einsum("bsd,bsf->df", hnorm_low, up_grad, preferred_element_type=jnp.float32)
    hnorm_part = jnp.einsum(
        "bsf,df->bsd", gate_grad, full_gate, preferred_element_type=jnp.float32
    ) + jnp.einsum("bsf,df->bsd", up_grad, full_up, preferred_element_type=jnp.float32)
    hnorm_grad = lax.psum(hnorm_part.astype(jnp.bfloat16), "tp").astype(jnp.float32)
    unused_norm, norm_pullback = jax.vjp(norm_rows, hidden, mlp_scale)
    hidden_back, mlp_gain_part = norm_pullback(hnorm_grad)
    hidden_grad = grad_float + hidden_back
    hidden_low = hidden_grad.astype(jnp.bfloat16)
    out_w_grad = jnp.einsum(
        "bse,bsd->ed", mixed_low, hidden_low, preferred_element_type=jnp.float32
    )
    attn_grad = jnp.einsum(
        "bsd,ed->bse", hidden_low, full_out, preferred_element_type=jnp.float32
    ).astype(jnp.bfloat16)
    attn_grad = attn_grad.reshape(block_len, seq_count, heads_local, HEAD_DIM)
    delta_rows = jnp.transpose(
        jnp.sum(attn_grad.astype(jnp.float32) * attn_exact, axis=-1), (1, 2, 0)
    )
    zero_query = jnp.zeros((block_len, seq_count, heads_local, HEAD_DIM), jnp.float32)

    def backward_shift(counter, loop_carry):
        query_acc, moving, travelling = loop_carry
        source = (ctx_index - counter) % ctx_size
        key_pos = block_positions(source, block_len, ctx_size)
        query_part, key_part = attend_back(
            queries, attn_grad, log_total, delta_rows, moving, prefix_len, query_pos, key_pos
        )
        travelling = pass_grads(travelling + key_part)
        moving = from_behind(moving, "ctx", 1)
        return (query_acc + query_part, moving, travelling)

    travel_zero = jnp.zeros((block_len, seq_count, heads_local, 2 * HEAD_DIM), jnp.float32)
    query_acc, moving, travelling = lax.fori_loop(
        0, ctx_size - 1, backward_shift, (zero_query, key_value, travel_zero)
    )
    last_source = (ctx_index + 1) % ctx_size
    last_pos = block_positions(last_source, block_len, ctx_size)
    query_part, key_part = attend_back(
        queries, attn_grad, log_total, delta_rows, moving, prefix_len, query_pos, last_pos
    )
    query_acc = query_acc + query_part
    own_grads = pass_grads(travelling + key_part)
    flat_shape = (block_len, seq_count, heads_local * HEAD_DIM)
    query_grad = unrotary(query_acc, cos_table, sine_table).astype(jnp.bfloat16).reshape(flat_shape)
    key_grad = (
        unrotary(own_grads[..., :HEAD_DIM], cos_table, sine_table)
        .astype(jnp.bfloat16)
        .reshape(flat_shape)
    )
    value_grad = own_grads[..., HEAD_DIM:].astype(jnp.bfloat16).reshape(flat_shape)
    query_w_grad = jnp.einsum(
        "bsd,bse->de", normed_low, query_grad, preferred_element_type=jnp.float32
    )
    key_w_grad = jnp.einsum("bsd,bse->de", normed_low, key_grad, preferred_element_type=jnp.float32)
    value_w_grad = jnp.einsum(
        "bsd,bse->de", normed_low, value_grad, preferred_element_type=jnp.float32
    )
    normed_part = (
        jnp.einsum("bse,de->bsd", query_grad, full_query, preferred_element_type=jnp.float32)
        + jnp.einsum("bse,de->bsd", key_grad, full_key, preferred_element_type=jnp.float32)
        + jnp.einsum("bse,de->bsd", value_grad, full_value, preferred_element_type=jnp.float32)
    )
    normed_grad = lax.psum(normed_part.astype(jnp.bfloat16), "tp").astype(jnp.float32)
    unused_first, first_pullback = jax.vjp(norm_rows, inputs, attn_scale)
    input_back, attn_gain_part = first_pullback(normed_grad)
    input_grad = (hidden_grad + input_back).astype(jnp.bfloat16)
    returned = mirror_rows(jnp.stack([layer_output[half_len:], input_grad[half_len:]], axis=0))
    layer_output = jnp.concatenate([layer_output[:half_len], returned[0]], axis=0)
    input_grad = jnp.concatenate([input_grad[:half_len], returned[1]], axis=0)
    shards = (
        lax.psum_scatter(
            attn_gain_part.astype(jnp.bfloat16), "fsdp", scatter_dimension=0, tiled=True
        ).astype(jnp.float32),
        lax.psum_scatter(
            mlp_gain_part.astype(jnp.bfloat16), "fsdp", scatter_dimension=0, tiled=True
        ).astype(jnp.float32),
        lax.psum_scatter(
            query_w_grad.astype(jnp.bfloat16), "fsdp", scatter_dimension=0, tiled=True
        ).astype(jnp.float32),
        lax.psum_scatter(
            key_w_grad.astype(jnp.bfloat16), "fsdp", scatter_dimension=0, tiled=True
        ).astype(jnp.float32),
        lax.psum_scatter(
            value_w_grad.astype(jnp.bfloat16), "fsdp", scatter_dimension=0, tiled=True
        ).astype(jnp.float32),
        lax.psum_scatter(
            out_w_grad.astype(jnp.bfloat16), "fsdp", scatter_dimension=1, tiled=True
        ).astype(jnp.float32),
        lax.psum_scatter(
            gate_w_grad.astype(jnp.bfloat16), "fsdp", scatter_dimension=0, tiled=True
        ).astype(jnp.float32),
        lax.psum_scatter(
            up_w_grad.astype(jnp.bfloat16), "fsdp", scatter_dimension=0, tiled=True
        ).astype(jnp.float32),
        lax.psum_scatter(
            down_w_grad.astype(jnp.bfloat16), "fsdp", scatter_dimension=1, tiled=True
        ).astype(jnp.float32),
    )
    totals = (
        lax.psum(shards[0].astype(jnp.bfloat16), "ctx").astype(jnp.float32),
        lax.psum(shards[1].astype(jnp.bfloat16), "ctx").astype(jnp.float32),
        lax.psum(shards[2].astype(jnp.bfloat16), "ctx").astype(jnp.float32),
        lax.psum(shards[3].astype(jnp.bfloat16), "ctx").astype(jnp.float32),
        lax.psum(shards[4].astype(jnp.bfloat16), "ctx").astype(jnp.float32),
        lax.psum(shards[5].astype(jnp.bfloat16), "ctx").astype(jnp.float32),
        lax.psum(shards[6].astype(jnp.bfloat16), "ctx").astype(jnp.float32),
        lax.psum(shards[7].astype(jnp.bfloat16), "ctx").astype(jnp.float32),
        lax.psum(shards[8].astype(jnp.bfloat16), "ctx").astype(jnp.float32),
    )
    return (
        layer_output,
        input_grad,
        totals[0],
        totals[1],
        totals[2],
        totals[3],
        totals[4],
        totals[5],
        totals[6],
        totals[7],
        totals[8],
    )


def solution(mesh):
    placed = (
        P("ctx", "fsdp", None),
        P("ctx", "fsdp", None),
        P("fsdp"),
        P("fsdp"),
        P("fsdp"),
        P("fsdp", "tp"),
        P("fsdp", "tp"),
        P("fsdp", "tp"),
        P("tp", "fsdp"),
        P("fsdp", "tp"),
        P("fsdp", "tp"),
        P("tp", "fsdp"),
    )
    return jax.shard_map(
        body,
        mesh=mesh,
        in_specs=placed,
        out_specs=(
            P("ctx", "fsdp", None),
            P("ctx", "fsdp", None),
            P("fsdp"),
            P("fsdp"),
            P("fsdp", "tp"),
            P("fsdp", "tp"),
            P("fsdp", "tp"),
            P("tp", "fsdp"),
            P("fsdp", "tp"),
            P("fsdp", "tp"),
            P("tp", "fsdp"),
        ),
        check_vma=False,
    )
```

profile of v0, /device:TPU:0, one launch (start us, length us, event | category | flops | bytes accessed | tf_op | source)
XLA Modules:
  0.0 1112.3 jit_solution(16232796103157032152)
XLA Ops:
  22.0 28.5 %collective-permute-done.3 = bf16[2,256,2,768]{3,1,2,0:T(8,128)(2,1)} collective-permute-done((bf16[2,256,2,768]{3,1,2,0:T(8,128)(2,1)S(1)}, bf16[2,256,2,768]{3,1,2,0:T(8,128)(2,1)}, u32[]{:S(2)}, u32[]{:S(2)}) %collective-permute-start.3) | collective-permute-done | bytes 1572896 | tf_op jit(solution)/shard_map/ppermute | solution.py:23
  60.3 12.5 %all-reduce.7 = (bf16[768]{0:T(1024)(128)(2,1)}, bf16[768]{0:T(1024)(128)(2,1)}) all-reduce(bf16[768]{0:T(1024)(128)(2,1)S(1)} %dynamic-update-slice, bf16[768]{0:T(1024)(128)(2,1)S(1)} %dynamic-update-slice.1), channel_id=1, replica_groups=mesh['fsdp'=4,'ctx'=4,'tp'=2] {'fsdp'}, use_global_device_ids=true, to_apply=%add | all-reduce | flops 1536 | bytes 6144
  74.2 15.7 %all_gather.31 = bf16[384,768]{0,1:T(8,128)(2,1)} all-gather(bf16[384,192]{0,1:T(8,128)(2,1)S(1)} %convert_element_type.280), channel_id=1, replica_groups=mesh['fsdp'=4,'ctx'=4,'tp'=2] {'fsdp'}, dimensions={1}, use_global_device_ids=true | all-gather | bytes 737280 | tf_op jit(solution)/shard_map/all_gather | solution.py:187
  89.9 16.1 %all_gather.30 = bf16[768,384]{1,0:T(8,128)(2,1)S(1)} all-gather(bf16[192,384]{1,0:T(8,128)(2,1)S(1)} %convert_element_type.275), channel_id=1, replica_groups=mesh['fsdp'=4,'ctx'=4,'tp'=2] {'fsdp'}, dimensions={0}, use_global_device_ids=true | all-gather | bytes 737280 | tf_op jit(solution)/shard_map/all_gather | solution.py:186
  106.0 16.6 %all_gather.29 = bf16[768,384]{1,0:T(8,128)(2,1)S(1)} all-gather(bf16[192,384]{1,0:T(8,128)(2,1)S(1)} %convert_element_type.273), channel_id=1, replica_groups=mesh['fsdp'=4,'ctx'=4,'tp'=2] {'fsdp'}, dimensions={0}, use_global_device_ids=true | all-gather | bytes 737280 | tf_op jit(solution)/shard_map/all_gather | solution.py:185
  122.6 15.0 %all_gather.28 = bf16[768,384]{1,0:T(8,128)(2,1)S(1)} all-gather(bf16[192,384]{1,0:T(8,128)(2,1)S(1)} %convert_element_type.270), channel_id=1, replica_groups=mesh['fsdp'=4,'ctx'=4,'tp'=2] {'fsdp'}, dimensions={0}, use_global_device_ids=true | all-gather | bytes 737280 | tf_op jit(solution)/shard_map/all_gather | solution.py:184
  147.4 13.1 %conditional.4 = (f32[2,6,512]{2,1,0:T(8,128)}, f32[2,6,512]{2,1,0:T(8,128)S(1)}, f32[512,2,6,64]{0,3,2,1:T(8,128)}) conditional(s32[]{:T(128)} %convert_element_type.266, () %tuple.85, (s32[512]{0:T(512)S(1)}, s32[2]{0:T(128)S(1)}, bf16[512,2,6,64]{0,3,2,1:T(8,128)(2,1)S(1)}, bf16[512,2,6,64]{0,3,2,1:T(8,128)(2,1)S(1)}, ...), branch_computations={%region_6.0_spmd, %region_7.10_spmd} | conditional | flops 841114624 | bytes 51918964 | solution.py:112
  160.5 123.5 %while.41 = (s32[]{:T(128)}, f32[2,6,512]{2,1,0:T(8,128)}, f32[2,6,512]{2,1,0:T(8,128)S(1)}, f32[512,2,6,64]{0,3,2,1:T(8,128)}, bf16[512,2,6,128]{0,3,2,1:T(8,12...) while((s32[]{:T(128)}, f32[2,6,512]{2,1,0:T(8,128)}, ...), condition=%wide.region_18.19_spmd, body=%wide.region_10.18_spmd.sunk | while | flops 841503744 | bytes 55720504 | solution.py:224
  165.5 20.6 %collective-permute-done = bf16[512,2,6,128]{0,3,2,1:T(8,128)(2,1)} collective-permute-done((bf16[512,2,6,128]{0,3,2,1:T(8,128)(2,1)}, bf16[512,2,6,128]{0,3,2,1:T(8,128)(2,1)}, u32[]{:S(2)}, u32[]{:S(2)}) %collective-permute-start) | collective-permute-done | bytes 1572896 | tf_op jit(solution)/shard_map/while/body/eval_jaxpr/ppermute | solution.py:29
  186.1 13.9 %conditional.9 = ((f32[2,6,512]{2,1,0:T(8,128)}, f32[2,6,512]{2,1,0:T(8,128)S(1)}, f32[512,2,6,64]{0,3,2,1:T(8,128)})) conditional(s32[]{:T(128)} %convert_element_type.485, (f32[2,6,512]{2,1,0:T(8,128)}, f32[2,6,512]{2,1,0:T(8,128)S(1)}, f32[512,2,6,64]{0,3,2,1:T(8,128)}) %tuple.162, (s32[512]{0:T(512)S(1)}, s32[512]{0:T(512)S(1)}, ...), branch_computations={%region_14.14_spmd, %region_15.0_spmd} | conditional | flops 841501696 | bytes 46276648 | solution.py:112
  206.6 20.7 %collective-permute-done = bf16[512,2,6,128]{0,3,2,1:T(8,128)(2,1)} collective-permute-done((bf16[512,2,6,128]{0,3,2,1:T(8,128)(2,1)}, bf16[512,2,6,128]{0,3,2,1:T(8,128)(2,1)}, u32[]{:S(2)}, u32[]{:S(2)}) %collective-permute-start) | collective-permute-done | bytes 1572896 | tf_op jit(solution)/shard_map/while/body/eval_jaxpr/ppermute | solution.py:29
  227.2 13.9 %conditional.9 = ((f32[2,6,512]{2,1,0:T(8,128)}, f32[2,6,512]{2,1,0:T(8,128)S(1)}, f32[512,2,6,64]{0,3,2,1:T(8,128)})) conditional(s32[]{:T(128)} %convert_element_type.485, (f32[2,6,512]{2,1,0:T(8,128)}, f32[2,6,512]{2,1,0:T(8,128)S(1)}, f32[512,2,6,64]{0,3,2,1:T(8,128)}) %tuple.162, (s32[512]{0:T(512)S(1)}, s32[512]{0:T(512)S(1)}, ...), branch_computations={%region_14.14_spmd, %region_15.0_spmd} | conditional | flops 841501696 | bytes 46276648 | solution.py:112
  247.1 20.4 %collective-permute-done = bf16[512,2,6,128]{0,3,2,1:T(8,128)(2,1)} collective-permute-done((bf16[512,2,6,128]{0,3,2,1:T(8,128)(2,1)}, bf16[512,2,6,128]{0,3,2,1:T(8,128)(2,1)}, u32[]{:S(2)}, u32[]{:S(2)}) %collective-permute-start) | collective-permute-done | bytes 1572896 | tf_op jit(solution)/shard_map/while/body/eval_jaxpr/ppermute | solution.py:29
  267.5 13.9 %conditional.9 = ((f32[2,6,512]{2,1,0:T(8,128)}, f32[2,6,512]{2,1,0:T(8,128)S(1)}, f32[512,2,6,64]{0,3,2,1:T(8,128)})) conditional(s32[]{:T(128)} %convert_element_type.485, (f32[2,6,512]{2,1,0:T(8,128)}, f32[2,6,512]{2,1,0:T(8,128)S(1)}, f32[512,2,6,64]{0,3,2,1:T(8,128)}) %tuple.162, (s32[512]{0:T(512)S(1)}, s32[512]{0:T(512)S(1)}, ...), branch_computations={%region_14.14_spmd, %region_15.0_spmd} | conditional | flops 841501696 | bytes 46276648 | solution.py:112
  294.2 6.3 fusion.79
  300.5 8.9 all-reduce.14.cloned.1.call-done
  313.3 15.5 %all-gather.4.cloned.1.call-done = bf16[768,1024]{1,0:T(8,128)(2,1)} async-done(((bf16[192,1024]{1,0:T(8,128)(2,1)}), bf16[768,1024]{1,0:T(8,128)(2,1)}) %all-gather.4.cloned.1.call-update) | async-done | bytes 1572880 | tf_op jit(solution)/shard_map/all_gather | solution.py:191
  328.8 5.7 fusion.87
  334.5 31.8 %all-gather.6.cloned.1.call-done = bf16[768,1024]{1,0:T(8,128)(2,1)} async-done(((bf16[192,1024]{1,0:T(8,128)(2,1)}), bf16[768,1024]{1,0:T(8,128)(2,1)}) %all-gather.6.cloned.1.call-update) | async-done | bytes 1572880 | tf_op jit(solution)/shard_map/all_gather | solution.py:192
  366.3 9.0 multiply_convert_fusion.3
  382.9 16.9 %all-reduce.16.cloned.1.call-done = bf16[512,2,768]{2,0,1:T(8,128)(2,1)} async-done(((bf16[512,2,768]{2,0,1:T(8,128)(2,1)}), bf16[512,2,768]{2,0,1:T(8,128)(2,1)}) %all-reduce.16.cloned.1.call-update) | async-done | bytes 1572880 | tf_op jit(solution)/shard_map/psum | solution.py:263
  404.1 14.6 %fusion.93 = bf16[512,2,768]{2,0,1:T(8,128)(2,1)S(1)} fusion(f32[512,2]{0,1:T(2,128)S(1)} %multiply_multiply_fusion.1, bf16[512,2,768]{2,0,1:T(8,128)(2,1)S(1)} %copy-done.11, f32[512,2]{0,1:T(2,128)S(1)} %fusion.108, f32[768]{0:T(1024)S(1)} %convert_element_type.284, bf16[512,2,768]{2,0,1:T(8,128)(2,1)S(1)} %copy-done.14, ...), kind=kLoop, calls=%fused_computation.168 | loop fusion | flops 14155776 | bytes 7875584 | tf_op jit(solution)/shard_map/convert_element_type | solution.py:267
  421.3 298.5 %while.42 = (s32[]{:T(128)}, f32[512,2,6,64]{0,3,2,1:T(8,128)}, bf16[512,2,6,128]{0,3,2,1:T(8,128)(2,1)}, f32[512,2,6,128]{0,3,2,1:T(8,128)}, s32[]{:T(128)}, /*...) while((s32[]{:T(128)}, f32[512,2,6,64]{0,3,2,1:T(8,128)}, ...), condition=%wide.region_31.32_spmd.clone, body=%wide.region_25.31_spmd.clone.sunk | while | flops 2051017216 | bytes 133520112 | solution.py:292
  428.0 18.4 %conditional.10 = (f32[512,2,6,64]{0,3,2,1:T(8,128)S(1)}, f32[512,2,6,128]{0,3,2,1:T(8,128)S(1)}) conditional(s32[]{:T(128)} %convert_element_type.487, () %tuple.167, (s32[512]{0:T(512)S(1)}, s32[512]{0:T(512)S(1)}, s32[2]{0:T(128)S(1)}, bf16[512,2,6,128]{0,3,2,1:T(8,128)(2,1)}, bf16[512,2,6,64]{0,3,2,1:T(8,128)(2,1)S(1)}, ...), branch_computations={%region_29.29_spmd, %region_30.30_spmd} | conditional | flops 2047083520 | bytes 81608752 | solution.py:152
  435.4 6.2 multiply_convert_fusion
  454.7 32.3 %collective-permute-done.2 = bf16[512,2,6,128]{0,3,2,1:T(8,128)(2,1)} collective-permute-done((bf16[512,2,6,128]{0,3,2,1:T(8,128)(2,1)}, bf16[512,2,6,128]{0,3,2,1:T(8,128)(2,1)}, u32[]{:S(2)}, u32[]{:S(2)}) %collective-permute-start.2) | collective-permute-done | bytes 1572896 | tf_op jit(solution)/shard_map/while/body/eval_jaxpr/ppermute | solution.py:29
  490.4 29.6 %collective-permute-done.1 = bf16[512,2,6,128]{0,3,2,1:T(8,128)(2,1)} collective-permute-done((bf16[512,2,6,128]{0,3,2,1:T(8,128)(2,1)}, bf16[512,2,6,128]{0,3,2,1:T(8,128)(2,1)}, u32[]{:S(2)}, u32[]{:S(2)}) %collective-permute-start.1) | collective-permute-done | bytes 1572896 | tf_op jit(solution)/shard_map/while/body/eval_jaxpr/ppermute | solution.py:29
  526.7 18.5 %conditional.10 = (f32[512,2,6,64]{0,3,2,1:T(8,128)S(1)}, f32[512,2,6,128]{0,3,2,1:T(8,128)S(1)}) conditional(s32[]{:T(128)} %convert_element_type.487, () %tuple.167, (s32[512]{0:T(512)S(1)}, s32[512]{0:T(512)S(1)}, s32[2]{0:T(128)S(1)}, bf16[512,2,6,128]{0,3,2,1:T(8,128)(2,1)}, bf16[512,2,6,64]{0,3,2,1:T(8,128)(2,1)S(1)}, ...), branch_computations={%region_29.29_spmd, %region_30.30_spmd} | conditional | flops 2047083520 | bytes 81608752 | solution.py:152
  534.1 6.2 multiply_convert_fusion
  556.3 31.9 %collective-permute-done.2 = bf16[512,2,6,128]{0,3,2,1:T(8,128)(2,1)} collective-permute-done((bf16[512,2,6,128]{0,3,2,1:T(8,128)(2,1)}, bf16[512,2,6,128]{0,3,2,1:T(8,128)(2,1)}, u32[]{:S(2)}, u32[]{:S(2)}) %collective-permute-start.2) | collective-permute-done | bytes 1572896 | tf_op jit(solution)/shard_map/while/body/eval_jaxpr/ppermute | solution.py:29
  591.6 28.7 %collective-permute-done.1 = bf16[512,2,6,128]{0,3,2,1:T(8,128)(2,1)} collective-permute-done((bf16[512,2,6,128]{0,3,2,1:T(8,128)(2,1)}, bf16[512,2,6,128]{0,3,2,1:T(8,128)(2,1)}, u32[]{:S(2)}, u32[]{:S(2)}) %collective-permute-start.1) | collective-permute-done | bytes 1572896 | tf_op jit(solution)/shard_map/while/body/eval_jaxpr/ppermute | solution.py:29
  627.0 18.5 %conditional.10 = (f32[512,2,6,64]{0,3,2,1:T(8,128)S(1)}, f32[512,2,6,128]{0,3,2,1:T(8,128)S(1)}) conditional(s32[]{:T(128)} %convert_element_type.487, () %tuple.167, (s32[512]{0:T(512)S(1)}, s32[512]{0:T(512)S(1)}, s32[2]{0:T(128)S(1)}, bf16[512,2,6,128]{0,3,2,1:T(8,128)(2,1)}, bf16[512,2,6,64]{0,3,2,1:T(8,128)(2,1)S(1)}, ...), branch_computations={%region_29.29_spmd, %region_30.30_spmd} | conditional | flops 2047083520 | bytes 81608752 | solution.py:152
  634.4 6.2 multiply_convert_fusion
  656.5 31.9 %collective-permute-done.2 = bf16[512,2,6,128]{0,3,2,1:T(8,128)(2,1)} collective-permute-done((bf16[512,2,6,128]{0,3,2,1:T(8,128)(2,1)}, bf16[512,2,6,128]{0,3,2,1:T(8,128)(2,1)}, u32[]{:S(2)}, u32[]{:S(2)}) %collective-permute-start.2) | collective-permute-done | bytes 1572896 | tf_op jit(solution)/shard_map/while/body/eval_jaxpr/ppermute | solution.py:29
  691.9 27.9 %collective-permute-done.1 = bf16[512,2,6,128]{0,3,2,1:T(8,128)(2,1)} collective-permute-done((bf16[512,2,6,128]{0,3,2,1:T(8,128)(2,1)}, bf16[512,2,6,128]{0,3,2,1:T(8,128)(2,1)}, u32[]{:S(2)}, u32[]{:S(2)}) %collective-permute-start.1) | collective-permute-done | bytes 1572896 | tf_op jit(solution)/shard_map/while/body/eval_jaxpr/ppermute | solution.py:29
  719.8 18.9 %conditional.5 = (f32[512,2,6,64]{0,3,2,1:T(8,128)S(1)}, f32[512,2,6,128]{0,3,2,1:T(8,128)S(1)}) conditional(s32[]{:T(128)} %convert_element_type.301, () %tuple.89, (s32[512]{0:T(512)S(1)}, s32[512]{0:T(512)S(1)}, s32[2]{0:T(128)S(1)}, bf16[512,2,6,128]{0,3,2,1:T(8,128)(2,1)}, bf16[512,2,6,64]{0,3,2,1:T(8,128)(2,1)S(1)}, ...), branch_computations={%region_35.36_spmd, %region_36.37_spmd} | conditional | flops 2047083520 | bytes 81608752 | solution.py:152
  727.2 6.2 multiply_convert_fusion.1
  744.6 31.6 %collective-permute-done.5 = bf16[512,2,6,128]{0,3,2,1:T(8,128)(2,1)S(1)} collective-permute-done((bf16[512,2,6,128]{0,3,2,1:T(8,128)(2,1)S(1)}, bf16[512,2,6,128]{0,3,2,1:T(8,128)(2,1)S(1)}, u32[]{:S(2)}, u32[]{:S(2)}) %collective-permute-start.5) | collective-permute-done | bytes 1572896 | tf_op jit(solution)/shard_map/ppermute | solution.py:29
  791.8 5.6 bitcast_convert_fusion.1
  819.6 26.0 %reduce-scatter.20.cloned.1.call-done = bf16[1024,192]{0,1:T(8,128)(2,1)} async-done(((bf16[1024,768]{0,1:T(8,128)(2,1)}), bf16[1024,192]{0,1:T(8,128)(2,1)}) %reduce-scatter.20.cloned.1.call-update) | async-done | bytes 393232 | tf_op jit(solution)/shard_map/reduce_scatter | solution.py:354
  845.6 36.5 %reduce-scatter.18.cloned.1.call-done = bf16[192,1024]{1,0:T(8,128)(2,1)} async-done(((bf16[768,1024]{1,0:T(8,128)(2,1)}), bf16[192,1024]{1,0:T(8,128)(2,1)}) %reduce-scatter.18.cloned.1.call-update) | async-done | bytes 393232 | tf_op jit(solution)/shard_map/reduce_scatter | solution.py:351
  882.1 36.6 %reduce-scatter.16.cloned.1.call-done = bf16[192,1024]{1,0:T(8,128)(2,1)} async-done(((bf16[768,1024]{1,0:T(8,128)(2,1)}), bf16[192,1024]{1,0:T(8,128)(2,1)}) %reduce-scatter.16.cloned.1.call-update) | async-done | bytes 393232 | tf_op jit(solution)/shard_map/reduce_scatter | solution.py:348
  918.7 23.3 %reduce-scatter.12.cloned.1.call-done = bf16[192,384]{1,0:T(8,128)(2,1)} async-done(((bf16[768,384]{1,0:T(8,128)(2,1)}), bf16[192,384]{1,0:T(8,128)(2,1)}) %reduce-scatter.12.cloned.1.call-update) | async-done | bytes 147472 | tf_op jit(solution)/shard_map/reduce_scatter | solution.py:342
  942.0 23.5 %reduce-scatter.8.cloned.1.call-done = bf16[192,384]{1,0:T(8,128)(2,1)} async-done(((bf16[768,384]{1,0:T(8,128)(2,1)}), bf16[192,384]{1,0:T(8,128)(2,1)}) %reduce-scatter.8.cloned.1.call-update) | async-done | bytes 147472 | tf_op jit(solution)/shard_map/reduce_scatter | solution.py:336
  965.5 23.3 %reduce-scatter.10.cloned.1.call-done = bf16[192,384]{1,0:T(8,128)(2,1)} async-done(((bf16[768,384]{1,0:T(8,128)(2,1)}), bf16[192,384]{1,0:T(8,128)(2,1)}) %reduce-scatter.10.cloned.1.call-update) | async-done | bytes 147472 | tf_op jit(solution)/shard_map/reduce_scatter | solution.py:339
  991.1 74.9 %all-reduce.18.cloned.1.call-done = (bf16[192,384]{1,0:T(8,128)(2,1)}, bf16[192,384]{1,0:T(8,128)(2,1)}, bf16[192,384]{1,0:T(8,128)(2,1)}, bf16[384,192]{0,1:T(8...) async-done(((bf16[192,384]{1,0:T(8,128)(2,1)}, bf16[192,384]{1,0:T(8,128)(2,1)}, bf16[192,384]{1,0:T(8,128)(2,1)}, ...) | async-done | bytes 1769488 | tf_op jit(solution)/shard_map/psum | solution.py:361
  1076.5 11.7 %all-reduce.6 = (bf16[768]{0:T(1024)(128)(2,1)S(1)}, bf16[768]{0:T(1024)(128)(2,1)S(1)}) all-reduce(bf16[768]{0:T(1024)(128)(2,1)S(1)} %get-tuple-element.729, bf16[768]{0:T(1024)(128)(2,1)S(1)} %copy-done.63), channel_id=2, replica_groups=mesh['fsdp'=4,'ctx'=4,'tp'=2] {'fsdp'}, use_global_device_ids=true, to_apply=%region_40.41.clone | all-reduce | flops 1536 | bytes 6144
  1088.4 9.1 all-reduce.4
  (423 shorter events, 291.7 us)
Async XLA Ops:
  8.0 286.2 %all-gather.8.cloned.1.call-start = ((), (), s32[]{:S(2)}) async-start(), calls=%async_computation.10 | async-start | bytes 1966080 | tf_op jit(solution)/shard_map/all_gather | solution.py:193
  12.8 40.2 %copy-start.70 = (f32[192]{0:T(256)S(1)}, f32[192]{0:T(256)}, u32[]{:S(2)}) copy-start(f32[192]{0:T(256)} %param.27) | copy-start | bytes 2308
  12.8 44.5 %copy-start.66 = (u32[32]{0:T(128)S(1)}, u32[32]{0:T(128)}, u32[]{:S(2)}) copy-start(u32[32]{0:T(128)} %constant.297) | copy-start | bytes 388
  12.8 60.7 %copy-start.45 = (f32[192,384]{1,0:T(8,128)S(1)}, f32[192,384]{1,0:T(8,128)}, u32[]{:S(2)}) copy-start(f32[192,384]{1,0:T(8,128)} %param.29) | copy-start | bytes 884740
  12.9 60.7 %copy-start.46 = (f32[192,384]{1,0:T(8,128)S(1)}, f32[192,384]{1,0:T(8,128)}, u32[]{:S(2)}) copy-start(f32[192,384]{1,0:T(8,128)} %param.30) | copy-start | bytes 884740
  12.9 60.7 %copy-start.47 = (f32[192,384]{1,0:T(8,128)S(1)}, f32[192,384]{1,0:T(8,128)}, u32[]{:S(2)}) copy-start(f32[192,384]{1,0:T(8,128)} %param.31) | copy-start | bytes 884740
  12.9 60.7 %copy-start.48 = (f32[384,192]{0,1:T(8,128)S(1)}, f32[384,192]{0,1:T(8,128)}, u32[]{:S(2)}) copy-start(f32[384,192]{0,1:T(8,128)} %param.32) | copy-start | bytes 884740
  13.0 37.5 %collective-permute-start.3 = (bf16[2,256,2,768]{3,1,2,0:T(8,128)(2,1)S(1)}, bf16[2,256,2,768]{3,1,2,0:T(8,128)(2,1)}, u32[]{:S(2)}, u32[]{:S(2)}) collective-permute-start(bf16[2,256,2,768]{3,1,2,0:T(8,128)(2,1)S(1)} %pad_maximum_fusion.2), channel_id=1, source_target_pairs={{0,2},{2,0},{4,6},{6,4},{1,3},{3,1},{5,7},{7,5},{8,10},{10,8},{12,... | collective-permute-start | bytes 4718600 | tf_op jit(solution)/shard_map/ppermute | solution.py:23
  16.9 292.5 %all-reduce.14.cloned.1.call-start = ((), (), s32[]{:S(2)}) async-start(), calls=%async_computation.7 | async-start | bytes 3145728 | tf_op jit(solution)/shard_map/psum | solution.py:234
  50.6 87.0 %collective-permute-start.4 = (bf16[2,256,2,768]{3,1,2,0:T(8,128)(2,1)}, bf16[2,256,2,768]{3,1,2,0:T(8,128)(2,1)S(1)}, u32[]{:S(2)}, u32[]{:S(2)}) collective-permute-start(bf16[2,256,2,768]{3,1,2,0:T(8,128)(2,1)} %collective-permute-done.3), channel_id=1, source_target_pairs={{0,4},{4,0},{2,6},{6,2},{1,5},{5,1},{3,7},{7,3},{8,12},{12,8},{10,... | collective-permute-start | bytes 4718600 | tf_op jit(solution)/shard_map/ppermute | solution.py:23
  73.5 68.0 %copy-start.56 = (f32[768]{0:T(1024)}, f32[768]{0:T(1024)S(1)}, u32[]{:S(2)}) copy-start(f32[768]{0:T(1024)S(1)} %convert_element_type.268) | copy-start | bytes 9220
  73.7 67.7 %copy-start.4 = (bf16[256,2,768]{2,0,1:T(8,128)(2,1)}, bf16[256,2,768]{2,0,1:T(8,128)(2,1)S(1)}, u32[]{:S(2)}) copy-start(bf16[256,2,768]{2,0,1:T(8,128)(2,1)S(1)} %copy.108) | copy-start | bytes 2359300
  74.1 68.4 %copy-start.32 = (f32[512,64]{0,1:T(8,128)}, f32[512,64]{0,1:T(8,128)S(1)}, u32[]{:S(2)}) copy-start(f32[512,64]{0,1:T(8,128)S(1)} %pad_maximum_fusion.9) | copy-start | bytes 393220
  74.2 68.4 %copy-start.34 = (f32[512,64]{0,1:T(8,128)}, f32[512,64]{0,1:T(8,128)S(1)}, u32[]{:S(2)}) copy-start(f32[512,64]{0,1:T(8,128)S(1)} %pad_maximum_fusion.10) | copy-start | bytes 393220
  160.6 25.5 %collective-permute-start = (bf16[512,2,6,128]{0,3,2,1:T(8,128)(2,1)}, bf16[512,2,6,128]{0,3,2,1:T(8,128)(2,1)}, u32[]{:S(2)}, u32[]{:S(2)}) collective-permute-start(bf16[512,2,6,128]{0,3,2,1:T(8,128)(2,1)} %get-tuple-element.1055), channel_id=1, source_target_pairs={{0,2},{2,4},{4,6},{6,0},{1,3},{3,5},{5,7},{7,1},{8,10},{10,12},{12... | collective-permute-start | bytes 4718600 | tf_op jit(solution)/shard_map/while/body/eval_jaxpr/ppermute | solution.py:29
  202.6 24.6 %collective-permute-start = (bf16[512,2,6,128]{0,3,2,1:T(8,128)(2,1)}, bf16[512,2,6,128]{0,3,2,1:T(8,128)(2,1)}, u32[]{:S(2)}, u32[]{:S(2)}) collective-permute-start(bf16[512,2,6,128]{0,3,2,1:T(8,128)(2,1)} %get-tuple-element.1055), channel_id=1, source_target_pairs={{0,2},{2,4},{4,6},{6,0},{1,3},{3,5},{5,7},{7,1},{8,10},{10,12},{12... | collective-permute-start | bytes 4718600 | tf_op jit(solution)/shard_map/while/body/eval_jaxpr/ppermute | solution.py:29
  243.8 23.8 %collective-permute-start = (bf16[512,2,6,128]{0,3,2,1:T(8,128)(2,1)}, bf16[512,2,6,128]{0,3,2,1:T(8,128)(2,1)}, u32[]{:S(2)}, u32[]{:S(2)}) collective-permute-start(bf16[512,2,6,128]{0,3,2,1:T(8,128)(2,1)} %get-tuple-element.1055), channel_id=1, source_target_pairs={{0,2},{2,4},{4,6},{6,0},{1,3},{3,5},{5,7},{7,1},{8,10},{10,12},{12... | collective-permute-start | bytes 4718600 | tf_op jit(solution)/shard_map/while/body/eval_jaxpr/ppermute | solution.py:29
  290.0 38.8 %all-gather.4.cloned.1.call-start = ((), (), s32[]{:S(2)}) async-start(), calls=%async_computation.8 | async-start | bytes 1966080 | tf_op jit(solution)/shard_map/all_gather | solution.py:191
  290.9 75.4 %all-gather.6.cloned.1.call-start = ((), (), s32[]{:S(2)}) async-start(), calls=%async_computation.9 | async-start | bytes 1966080 | tf_op jit(solution)/shard_map/all_gather | solution.py:192
  292.9 107.0 %all-reduce.16.cloned.1.call-start = ((), (), s32[]{:S(2)}) async-start(), calls=%async_computation.11 | async-start | bytes 3145728 | tf_op jit(solution)/shard_map/psum | solution.py:263
  293.3 110.8 %copy-start.49 = (f32[768]{0:T(1024)}, f32[768]{0:T(1024)S(1)}, u32[]{:S(2)}) copy-start(f32[768]{0:T(1024)S(1)} %convert_element_type.284) | copy-start | bytes 9220
  311.6 92.4 %copy-start.51 = (f32[512,2]{0,1:T(2,128)}, f32[512,2]{0,1:T(2,128)S(1)}, u32[]{:S(2)}) copy-start(f32[512,2]{0,1:T(2,128)S(1)} %fusion.108) | copy-start | bytes 12292
  380.9 426.5 %all-reduce.20.cloned.1.call-start = ((), (), s32[]{:S(2)}) async-start(), calls=%async_computation.20 | async-start | bytes 6291456 | tf_op jit(solution)/shard_map/psum | solution.py:322
  421.3 298.5 %copy-start.62 = (s32[512]{0:T(512)S(1)}, s32[512]{0:T(512)}, u32[]{:S(2)}) copy-start(s32[512]{0:T(512)} %pad_add_fusion.3) | copy-start | bytes 6148
  448.5 38.5 %collective-permute-start.2 = (bf16[512,2,6,128]{0,3,2,1:T(8,128)(2,1)}, bf16[512,2,6,128]{0,3,2,1:T(8,128)(2,1)}, u32[]{:S(2)}, u32[]{:S(2)}) collective-permute-start(bf16[512,2,6,128]{0,3,2,1:T(8,128)(2,1)} %fusion.168), channel_id=1, source_target_pairs={{0,2},{2,4},{4,6},{6,0},{1,3},{3,5},{5,7},{7,1},{8,10},{10,12},{12... | collective-permute-start | bytes 4718600 | tf_op jit(solution)/shard_map/while/body/eval_jaxpr/ppermute | solution.py:29
  450.3 69.8 %collective-permute-start.1 = (bf16[512,2,6,128]{0,3,2,1:T(8,128)(2,1)}, bf16[512,2,6,128]{0,3,2,1:T(8,128)(2,1)}, u32[]{:S(2)}, u32[]{:S(2)}) collective-permute-start(bf16[512,2,6,128]{0,3,2,1:T(8,128)(2,1)} %copy.155), channel_id=1, source_target_pairs={{0,2},{2,4},{4,6},{6,0},{1,3},{3,5},{5,7},{7,1},{8,10},{10,12},{12... | collective-permute-start | bytes 4718600 | tf_op jit(solution)/shard_map/while/body/eval_jaxpr/ppermute | solution.py:29
  454.7 65.4 %copy-start.1 = (bf16[512,2,6,64]{0,3,2,1:T(8,128)(2,1)S(1)}, bf16[512,2,6,64]{0,3,2,1:T(8,128)(2,1)}, u32[]{:S(2)}) copy-start(bf16[512,2,6,64]{0,3,2,1:T(8,128)(2,1)} %copy-done) | copy-start | bytes 2359300 | tf_op jit(solution)/shard_map/while
  454.7 65.4 %copy-start.40 = (bf16[512,2,6,64]{0,3,2,1:T(8,128)(2,1)S(1)}, bf16[512,2,6,64]{0,3,2,1:T(8,128)(2,1)}, u32[]{:S(2)}) copy-start(bf16[512,2,6,64]{0,3,2,1:T(8,128)(2,1)} %copy-done.39) | copy-start | bytes 2359300 | tf_op jit(solution)/shard_map/while
  549.7 38.5 %collective-permute-start.2 = (bf16[512,2,6,128]{0,3,2,1:T(8,128)(2,1)}, bf16[512,2,6,128]{0,3,2,1:T(8,128)(2,1)}, u32[]{:S(2)}, u32[]{:S(2)}) collective-permute-start(bf16[512,2,6,128]{0,3,2,1:T(8,128)(2,1)} %fusion.168), channel_id=1, source_target_pairs={{0,2},{2,4},{4,6},{6,0},{1,3},{3,5},{5,7},{7,1},{8,10},{10,12},{12... | collective-permute-start | bytes 4718600 | tf_op jit(solution)/shard_map/while/body/eval_jaxpr/ppermute | solution.py:29
  550.5 69.9 %collective-permute-start.1 = (bf16[512,2,6,128]{0,3,2,1:T(8,128)(2,1)}, bf16[512,2,6,128]{0,3,2,1:T(8,128)(2,1)}, u32[]{:S(2)}, u32[]{:S(2)}) collective-permute-start(bf16[512,2,6,128]{0,3,2,1:T(8,128)(2,1)} %copy.155), channel_id=1, source_target_pairs={{0,2},{2,4},{4,6},{6,0},{1,3},{3,5},{5,7},{7,1},{8,10},{10,12},{12... | collective-permute-start | bytes 4718600 | tf_op jit(solution)/shard_map/while/body/eval_jaxpr/ppermute | solution.py:29
  556.2 64.1 %copy-start.1 = (bf16[512,2,6,64]{0,3,2,1:T(8,128)(2,1)S(1)}, bf16[512,2,6,64]{0,3,2,1:T(8,128)(2,1)}, u32[]{:S(2)}) copy-start(bf16[512,2,6,64]{0,3,2,1:T(8,128)(2,1)} %copy-done) | copy-start | bytes 2359300 | tf_op jit(solution)/shard_map/while
  556.2 64.1 %copy-start.40 = (bf16[512,2,6,64]{0,3,2,1:T(8,128)(2,1)S(1)}, bf16[512,2,6,64]{0,3,2,1:T(8,128)(2,1)}, u32[]{:S(2)}) copy-start(bf16[512,2,6,64]{0,3,2,1:T(8,128)(2,1)} %copy-done.39) | copy-start | bytes 2359300 | tf_op jit(solution)/shard_map/while
  650.0 38.5 %collective-permute-start.2 = (bf16[512,2,6,128]{0,3,2,1:T(8,128)(2,1)}, bf16[512,2,6,128]{0,3,2,1:T(8,128)(2,1)}, u32[]{:S(2)}, u32[]{:S(2)}) collective-permute-start(bf16[512,2,6,128]{0,3,2,1:T(8,128)(2,1)} %fusion.168), channel_id=1, source_target_pairs={{0,2},{2,4},{4,6},{6,0},{1,3},{3,5},{5,7},{7,1},{8,10},{10,12},{12... | collective-permute-start | bytes 4718600 | tf_op jit(solution)/shard_map/while/body/eval_jaxpr/ppermute | solution.py:29
  650.0 69.8 %collective-permute-start.1 = (bf16[512,2,6,128]{0,3,2,1:T(8,128)(2,1)}, bf16[512,2,6,128]{0,3,2,1:T(8,128)(2,1)}, u32[]{:S(2)}, u32[]{:S(2)}) collective-permute-start(bf16[512,2,6,128]{0,3,2,1:T(8,128)(2,1)} %copy.155), channel_id=1, source_target_pairs={{0,2},{2,4},{4,6},{6,0},{1,3},{3,5},{5,7},{7,1},{8,10},{10,12},{12... | collective-permute-start | bytes 4718600 | tf_op jit(solution)/shard_map/while/body/eval_jaxpr/ppermute | solution.py:29
  656.5 63.3 %copy-start.1 = (bf16[512,2,6,64]{0,3,2,1:T(8,128)(2,1)S(1)}, bf16[512,2,6,64]{0,3,2,1:T(8,128)(2,1)}, u32[]{:S(2)}) copy-start(bf16[512,2,6,64]{0,3,2,1:T(8,128)(2,1)} %copy-done) | copy-start | bytes 2359300 | tf_op jit(solution)/shard_map/while
  656.5 63.3 %copy-start.40 = (bf16[512,2,6,64]{0,3,2,1:T(8,128)(2,1)S(1)}, bf16[512,2,6,64]{0,3,2,1:T(8,128)(2,1)}, u32[]{:S(2)}) copy-start(bf16[512,2,6,64]{0,3,2,1:T(8,128)(2,1)} %copy-done.39) | copy-start | bytes 2359300 | tf_op jit(solution)/shard_map/while
  741.3 35.0 %collective-permute-start.5 = (bf16[512,2,6,128]{0,3,2,1:T(8,128)(2,1)S(1)}, bf16[512,2,6,128]{0,3,2,1:T(8,128)(2,1)S(1)}, u32[]{:S(2)}, u32[]{:S(2)}) collective-permute-start(bf16[512,2,6,128]{0,3,2,1:T(8,128)(2,1)S(1)} %add_convert_fusion.1), channel_id=1, source_target_pairs={{0,2},{2,4},{4,6},{6,0},{1,3},{3,5},{5,7},{7,1},{8,10},{10,12},{12... | collective-permute-start | bytes 4718600 | tf_op jit(solution)/shard_map/ppermute | solution.py:29
  783.4 36.2 %reduce-scatter.14.cloned.1.call-start = ((), (), s32[]{:S(2)}) async-start(), calls=%async_computation.15 | async-start | bytes 737280 | tf_op jit(solution)/shard_map/reduce_scatter | solution.py:345
  787.1 58.5 %reduce-scatter.20.cloned.1.call-start = ((), (), s32[]{:S(2)}) async-start(), calls=%async_computation.18 | async-start | bytes 1966080 | tf_op jit(solution)/shard_map/reduce_scatter | solution.py:354
  791.8 90.3 %reduce-scatter.18.cloned.1.call-start = ((), (), s32[]{:S(2)}) async-start(), calls=%async_computation.17 | async-start | bytes 1966080 | tf_op jit(solution)/shard_map/reduce_scatter | solution.py:351
  797.4 121.2 %reduce-scatter.16.cloned.1.call-start = ((), (), s32[]{:S(2)}) async-start(), calls=%async_computation.16 | async-start | bytes 1966080 | tf_op jit(solution)/shard_map/reduce_scatter | solution.py:348
  802.9 139.1 %reduce-scatter.12.cloned.1.call-start = ((), (), s32[]{:S(2)}) async-start(), calls=%async_computation.14 | async-start | bytes 737280 | tf_op jit(solution)/shard_map/reduce_scatter | solution.py:342
  805.1 160.4 %reduce-scatter.8.cloned.1.call-start = ((), (), s32[]{:S(2)}) async-start(), calls=%async_computation.12 | async-start | bytes 737280 | tf_op jit(solution)/shard_map/reduce_scatter | solution.py:336
  807.3 181.5 %reduce-scatter.10.cloned.1.call-start = ((), (), s32[]{:S(2)}) async-start(), calls=%async_computation.13 | async-start | bytes 737280 | tf_op jit(solution)/shard_map/reduce_scatter | solution.py:339
  816.3 172.5 %collective-permute-start.6 = (bf16[2,256,2,768]{3,1,2,0:T(8,128)(2,1)}, bf16[2,256,2,768]{3,1,2,0:T(8,128)(2,1)}, u32[]{:S(2)}, u32[]{:S(2)}) collective-permute-start(bf16[2,256,2,768]{3,1,2,0:T(8,128)(2,1)} %pad_maximum_fusion.6), channel_id=1, source_target_pairs={{0,2},{2,0},{4,6},{6,4},{1,3},{3,1},{5,7},{7,5},{8,10},{10,8},{12,... | collective-permute-start | bytes 4718600 | tf_op jit(solution)/shard_map/ppermute | solution.py:23
  819.6 246.4 %all-reduce.18.cloned.1.call-start = ((), (), s32[]{:S(2)}) async-start(), calls=%async_computation.19 | async-start | bytes 3538944 | tf_op jit(solution)/shard_map/psum | solution.py:361
  988.8 87.8 %copy-start.63 = (bf16[768]{0:T(1024)(128)(2,1)S(1)}, bf16[768]{0:T(1024)(128)(2,1)}, u32[]{:S(2)}) copy-start(bf16[768]{0:T(1024)(128)(2,1)} %get-tuple-element.727) | copy-start | bytes 4612
  988.8 109.8 %collective-permute-start.7 = (bf16[2,256,2,768]{3,1,2,0:T(8,128)(2,1)}, bf16[2,256,2,768]{3,1,2,0:T(8,128)(2,1)S(1)}, u32[]{:S(2)}, u32[]{:S(2)}) collective-permute-start(bf16[2,256,2,768]{3,1,2,0:T(8,128)(2,1)} %collective-permute-done.6), channel_id=1, source_target_pairs={{0,4},{4,0},{2,6},{6,2},{1,5},{5,1},{3,7},{7,3},{8,12},{12,8},{10,... | collective-permute-start | bytes 4718600 | tf_op jit(solution)/shard_map/ppermute | solution.py:23
  (66 other events, 435.5 us)
Sparse Core Ops, SparseCore 0:
  17.0 37.3 all-gather.7
  292.3 36.4 all-gather.3
  330.4 35.8 all-gather.5
  787.2 22.2 reduce-scatter.13
  811.7 33.8 reduce-scatter.19
  847.8 34.2 reduce-scatter.17
  884.4 34.2 reduce-scatter.15
  921.0 20.9 reduce-scatter.11
  944.8 20.5 reduce-scatter.7
  968.2 20.5 reduce-scatter.9
Sparse Core Ops, SparseCore 1:
  290.0 19.4 all-reduce.13
  381.0 18.8 all-reduce.15
  783.5 23.2 all-reduce.19
  988.9 77.0 all-reduce.17
where the time goes:
time: 1120 us; the launch traced here: 1110 us
  waiting for transfers between devices  622 us (56%)
  matrix products  167 us (15%)
  other arithmetic  130 us (12%)
  blocking collectives  96.7 us (9%)
  local copies, waits for them, and re-layouts  39.8 us (4%)
  between operations  23.5 us (2%)
  starting transfers between devices  20.4 us (2%)
  loops' own time  13.2 us (1%)
    ppermute x10, waiting for transfers between devices, from_behind(): return lax.ppermute(value, axis, pairs)  276 us
    psum x1, waiting for transfers between devices, body(): lax.psum(shards[2].astype(jnp.bfloat16), 'ctx').astype(jnp.float32)  74.9 us
    reduce_scatter x1, waiting for transfers between devices, body(): lax.psum_scatter(gate_w_grad.astype(jnp.bfloat16), 'fsdp', scatter_dimens...  36.6 us
    reduce_scatter x1, waiting for transfers between devices, body(): lax.psum_scatter(up_w_grad.astype(jnp.bfloat16), 'fsdp', scatter_dimensio...  36.5 us
    all_gather x1, waiting for transfers between devices, body(): lax.all_gather(up_weight.astype(jnp.bfloat16), 'fsdp', axis=0, tiled=True)  31.8 us
    ppermute x4, waiting for transfers between devices, partner(): return lax.ppermute(block, axis, route)  28.5 us
    reduce_scatter x1, waiting for transfers between devices, body(): lax.psum_scatter(down_w_grad.astype(jnp.bfloat16), 'fsdp', scatter_dimens...  26 us
    dot_general x4, matrix products, compute(): jnp.einsum('qshd,kshd->shqk', attn_grad, value_heads, preferred_element_t...  24.7 us
  transfers between devices with their start and end apart: 28, of which 22 were waited for; matrix products, arithmetic and copies ran while one was open for 16% of the time, Pallas kernels for 0%

commit v1 on v0

--- a/solution.py
+++ b/solution.py
@@ -1,8 +1,11 @@
+import functools
 import math
 
 import jax
 import jax.numpy as jnp
 from jax import lax
+from jax.experimental import pallas as pl
+from jax.experimental.pallas import tpu as pltpu
 from jax.sharding import PartitionSpec as P
 
 HEAD_DIM = 64
@@ -381,6 +384,793 @@
     )
 
 
+MESH = pl.DeviceIdType.MESH
+VMEM_LIMIT = 60 << 20
+
+
+def place():
+    ctx = lax.axis_index("ctx")
+    along_x = ctx + 1 - 2 * lax.rem(ctx, 2)
+    along_y = lax.rem(ctx + 2, 4)
+    return lax.axis_index("fsdp"), ctx, along_x, along_y, 3 - ctx
+
+
+def greet(devices):
+    barrier = pltpu.get_barrier_semaphore()
+    for device in devices:
+        pl.semaphore_signal(barrier, inc=1, device_id=device, device_id_type=MESH)
+    pl.semaphore_wait(barrier, len(devices))
+
+
+def rows_at(block, rows):
+    return pl.ds(pl.multiple_of(block * rows, 16), rows)
+
+
+def send(source, target, send_sem, recv_sem, device):
+    return pltpu.make_async_remote_copy(
+        src_ref=source,
+        dst_ref=target,
+        send_sem=send_sem,
+        recv_sem=recv_sem,
+        device_id=device,
+        device_id_type=MESH,
+    )
+
+
+def column_chunks(shapes, widest):
+    chunks = []
+    for index, (rows, columns) in enumerate(shapes):
+        count = -(-columns // widest)
+        while columns % count or (columns // count) % 128:
+            count += 1
+        width = columns // count
+        chunks += [(index, rows // 4, part * width, width) for part in range(count)]
+    return [chunk + (number % 2,) for number, chunk in enumerate(chunks)]
+
+
+def gather_steps(chunks, shard_refs, full_refs, local_sem, send_sems, recv_sems):
+    fsdp, ctx, along_x, along_y, across = place()
+    last = lax.axis_size("fsdp") - 1
+
+    def region(chunk, shard, quarter):
+        index, rows, low, width, _ = chunk
+        return full_refs[index].at[rows_at(shard * 4 + quarter, rows), pl.ds(low, width)]
+
+    def pass_on(number, shard, quarter, kind, device, source=None):
+        target = region(chunks[number], shard, quarter)
+        return send(
+            target if source is None else source,
+            target,
+            send_sems.at[number, shard, kind],
+            recv_sems.at[number, shard, quarter],
+            device,
+        )
+
+    def own_source(number):
+        index, rows, low, width, _ = chunks[number]
+        return shard_refs[index].at[rows_at(ctx, rows), pl.ds(low, width)]
+
+    def arrived(number, shard, quarter):
+        pass_on(number, shard, quarter, 0, {"ctx": along_x}).wait_recv()
+
+    count = range(len(chunks))
+    up, down = {"fsdp": lax.rem(fsdp + 1, last + 1)}, {"fsdp": lax.rem(fsdp + last, last + 1)}
+    to_x, to_y = {"ctx": along_x}, {"ctx": along_y}
+
+    def begin():
+        for number in count:
+
+            @pl.when(fsdp < last)
+            def _(number=number):
+                pass_on(number, fsdp, ctx, 0, up, own_source(number)).start()
+
+            @pl.when(fsdp > 0)
+            def _(number=number):
+                pass_on(number, fsdp, ctx, 1, down, own_source(number)).start()
+
+        for index, shard_ref in enumerate(shard_refs):
+            rows = shard_ref.shape[0]
+            pltpu.make_async_copy(
+                shard_ref, full_refs[index].at[rows_at(fsdp, rows)], local_sem.at[index]
+            ).start()
+
+    def each(steps, act):
+        for sign in (-1, 1):
+            shard = fsdp + sign * steps
+
+            @pl.when((shard >= 0) & (shard <= last))
+            def _(sign=sign, shard=shard):
+                act(shard, sign)
+
+    def from_line(number, steps):
+        def act(shard, sign):
+            arrived(number, shard, ctx)
+            if sign < 0:
+
+                @pl.when(fsdp < last)
+                def _():
+                    pass_on(number, shard, ctx, 0, up).start()
+
+            else:
+
+                @pl.when(fsdp > 0)
+                def _():
+                    pass_on(number, shard, ctx, 1, down).start()
+
+            pass_on(number, shard, ctx, 2, to_x).start()
+            pass_on(number, shard, ctx, 3, to_y).start()
+
+        each(steps, act)
+
+    def to_corner(number, steps):
+        def act(shard, sign):
+            if chunks[number][-1] == 0:
+                arrived(number, shard, along_x)
+                pass_on(number, shard, along_x, 4, to_y).start()
+            else:
+                arrived(number, shard, along_y)
+                pass_on(number, shard, along_y, 4, to_x).start()
+
+        each(steps, act)
+
+    def finish():
+        for steps in range(1, last + 1):
+            for number in count:
+
+                def act(shard, sign, number=number):
+                    arrived(number, shard, along_y if chunks[number][-1] == 0 else along_x)
+                    arrived(number, shard, across)
+                    forward = fsdp < last if sign < 0 else fsdp > 0
+
+                    @pl.when(forward)
+                    def _():
+                        pass_on(number, shard, ctx, 0 if sign < 0 else 1, up).wait_send()
+
+                    for kind in (2, 3, 4):
+                        pass_on(number, shard, ctx, kind, to_x).wait_send()
+
+                each(steps, act)
+        for number in count:
+
+            @pl.when(fsdp < last)
+            def _(number=number):
+                pass_on(number, fsdp, ctx, 0, up, own_source(number)).wait_send()
+
+            @pl.when(fsdp > 0)
+            def _(number=number):
+                pass_on(number, fsdp, ctx, 1, down, own_source(number)).wait_send()
+
+        for index, shard_ref in enumerate(shard_refs):
+            rows = shard_ref.shape[0]
+            pltpu.make_async_copy(
+                shard_ref, full_refs[index].at[rows_at(fsdp, rows)], local_sem.at[index]
+            ).wait()
+
+    return begin, from_line, to_corner, finish
+
+
+def neighbours(fsdp, along_x, along_y):
+    size = lax.axis_size("fsdp")
+    return [
+        {"ctx": along_x},
+        {"ctx": along_y},
+        {"fsdp": lax.rem(fsdp + 1, size)},
+        {"fsdp": lax.rem(fsdp + size - 1, size)},
+    ]
+
+
+def gather_kernel(chunks, arrays, *refs):
+    shard_refs, full_refs = refs[:arrays], refs[arrays : 2 * arrays]
+    local_sem, send_sems, recv_sems = refs[2 * arrays :]
+    fsdp, ctx, along_x, along_y, across = place()
+    greet(neighbours(fsdp, along_x, along_y))
+    begin, from_line, to_corner, finish = gather_steps(
+        chunks, shard_refs, full_refs, local_sem, send_sems, recv_sems
+    )
+    begin()
+    last = lax.axis_size("fsdp") - 1
+    for steps in range(1, last + 2):
+        for number in range(len(chunks)):
+            if steps <= last:
+                from_line(number, steps)
+            if steps > 1:
+                to_corner(number, steps - 1)
+    finish()
+
+
+def gather_scratch(shards, chunks):
+    return [
+        pltpu.SemaphoreType.DMA((len(shards),)),
+        pltpu.SemaphoreType.DMA((len(chunks), 4, 5)),
+        pltpu.SemaphoreType.DMA((len(chunks), 4, 4)),
+    ]
+
+
+def gather_shards(shards, collective_id):
+    chunks = column_chunks([shard.shape for shard in shards], 512)
+    size = lax.axis_size("fsdp")
+    anywhere = pl.BlockSpec(memory_space=pl.ANY)
+    return pl.pallas_call(
+        functools.partial(gather_kernel, chunks, len(shards)),
+        out_shape=[
+            jax.ShapeDtypeStruct((size * shard.shape[0], shard.shape[1]), shard.dtype)
+            for shard in shards
+        ],
+        in_specs=[pl.BlockSpec(memory_space=pltpu.VMEM)] * len(shards),
+        out_specs=[anywhere] * len(shards),
+        scratch_shapes=gather_scratch(shards, chunks),
+        compiler_params=pltpu.CompilerParams(
+            collective_id=collective_id, has_side_effects=True, vmem_limit_bytes=VMEM_LIMIT
+        ),
+        name="gather_shards",
+    )(*shards)
+
+
+def reduce_kernel(chunks, arrays, *refs):
+    full_refs, out_refs = refs[:arrays], refs[arrays : 2 * arrays]
+    rest = refs[2 * arrays :]
+    count = len(chunks)
+    buffers = [rest[6 * number : 6 * number + 6] for number in range(count)]
+    load_sems, send_sems, recv_sems = rest[6 * count :]
+    fsdp, ctx, along_x, along_y, across = place()
+    size = lax.axis_size("fsdp")
+    others = [{"fsdp": lax.rem(fsdp + step, size)} for step in range(1, size)]
+    greet([{"ctx": along_x}, {"ctx": along_y}] + others)
+
+    def quarter_of(number, quarter):
+        index, rows, low, width, _ = chunks[number]
+        return full_refs[index].at[:, rows_at(quarter, rows), pl.ds(low, width)]
+
+    def result(number, quarter):
+        index, rows, low, width, _ = chunks[number]
+        return out_refs[index].at[rows_at(quarter, rows), pl.ds(low, width)]
+
+    def first_second(number):
+        return (along_x, along_y) if chunks[number][-1] == 0 else (along_y, along_x)
+
+    def exchange(number, part):
+        first, _ = first_second(number)
+        return send(
+            quarter_of(number, first if part == 0 else across),
+            buffers[number][1].at[part],
+            send_sems.at[number, part],
+            recv_sems.at[number, part],
+            {"ctx": first},
+        )
+
+    def load(number, part):
+        _, second = first_second(number)
+        return pltpu.make_async_copy(
+            quarter_of(number, ctx if part == 0 else second),
+            buffers[number][0].at[part],
+            load_sems.at[number, part],
+        )
+
+    def second_hop(number):
+        _, second = first_second(number)
+        return send(
+            buffers[number][2],
+            buffers[number][3],
+            send_sems.at[number, 2],
+            recv_sems.at[number, 2],
+            {"ctx": second},
+        )
+
+    def along_line(number, step):
+        return send(
+            buffers[number][4].at[lax.rem(fsdp + step, size)],
+            buffers[number][5].at[step - 1],
+            send_sems.at[number, 2 + step],
+            recv_sems.at[number, 2 + step],
+            others[step - 1],
+        )
+
+    def spread(number, quarter, kind, target):
+        place_there = result(number, quarter)
+        return send(
+            place_there,
+            place_there,
+            send_sems.at[number, 2 + size + kind],
+            recv_sems.at[number, 2 + size + kind],
+            {"ctx": target},
+        )
+
+    def stage(number, at):
+        first, second = first_second(number)
+        own, landed, passing, arrived, total, line = buffers[number]
+        if at == 0:
+            for part in (1, 0):
+                exchange(number, part).start()
+                load(number, part).start()
+        elif at == 1:
+            load(number, 1).wait()
+            exchange(number, 1).wait_recv()
+            passing[...] = (own[1].astype(jnp.float32) + landed[1].astype(jnp.float32)).astype(
+                jnp.bfloat16
+            )
+            second_hop(number).start()
+        elif at == 2:
+            load(number, 0).wait()
+            exchange(number, 0).wait_recv()
+            second_hop(number).wait_recv()
+            total[...] = (
+                own[0].astype(jnp.float32)
+                + landed[0].astype(jnp.float32)
+                + arrived[...].astype(jnp.float32)
+            ).astype(jnp.bfloat16)
+            for step in range(1, size):
+                along_line(number, step).start()
+        elif at == 3:
+            value = total[fsdp].astype(jnp.float32)
+            for step in range(1, size):
+                along_line(number, step).wait_recv()
+                value = value + line[step - 1].astype(jnp.float32)
+            index, rows, low, width, _ = chunks[number]
+            out_refs[index][rows_at(ctx, rows), pl.ds(low, width)] = value.astype(jnp.bfloat16)
+            spread(number, ctx, 0, first).start()
+            spread(number, ctx, 1, second).start()
+        elif at == 4:
+            spread(number, first, 0, first).wait_recv()
+            spread(number, first, 2, second).start()
+        else:
+            spread(number, second, 1, second).wait_recv()
+            spread(number, across, 2, second).wait_recv()
+            for part in (0, 1):
+                exchange(number, part).wait_send()
+            second_hop(number).wait_send()
+            for step in range(1, size):
+                along_line(number, step).wait_send()
+            for kind in range(3):
+                spread(number, ctx, kind, first).wait_send()
+
+    for number in range(count):
+        stage(number, 0)
+    lag = 2
+    for tick in range(count + 4 * lag):
+        for at in range(5, 0, -1):
+            number = tick - (at - 1) * lag
+            if 0 <= number < count:
+                stage(number, at)
+
+
+def reduce_grads(grads, collective_id):
+    size = lax.axis_size("fsdp")
+    shapes = [(grad.shape[0] // size, grad.shape[1]) for grad in grads]
+    chunks = column_chunks(shapes, 512)
+    anywhere = pl.BlockSpec(memory_space=pl.ANY)
+    scratch = []
+    for _, rows, _, width, _ in chunks:
+        block = (size, rows, width)
+        for shape in ((2,) + block, (2,) + block, block, block, block, (size - 1, rows, width)):
+            scratch.append(pltpu.VMEM(shape, jnp.bfloat16))
+    scratch += [
+        pltpu.SemaphoreType.DMA((len(chunks), 2)),
+        pltpu.SemaphoreType.DMA((len(chunks), size + 5)),
+        pltpu.SemaphoreType.DMA((len(chunks), size + 5)),
+    ]
+    return pl.pallas_call(
+        functools.partial(reduce_kernel, chunks, len(grads)),
+        out_shape=[jax.ShapeDtypeStruct(shape, jnp.bfloat16) for shape in shapes],
+        in_specs=[anywhere] * len(grads),
+        out_specs=[pl.BlockSpec(memory_space=pltpu.VMEM)] * len(grads),
+        scratch_shapes=scratch,
+        compiler_params=pltpu.CompilerParams(
+            collective_id=collective_id, has_side_effects=True, vmem_limit_bytes=VMEM_LIMIT
+        ),
+        name="reduce_grads",
+    )(*[grad.reshape(size, shape[0], shape[1]) for grad, shape in zip(grads, shapes)])
+
+
+def swap_kernel(arrays, *refs):
+    block_refs, out_ref = refs[:arrays], refs[arrays]
+    local_sems, send_sems, recv_sems = refs[arrays + 1 :]
+    fsdp, ctx, along_x, along_y, across = place()
+    targets = (across, along_x, along_y)
+    greet([{"ctx": target} for target in targets])
+    copies = []
+    for index, block_ref in enumerate(block_refs):
+        for number, target in enumerate(targets):
+            copy = send(
+                block_ref.at[target],
+                out_ref.at[index, ctx],
+                send_sems.at[index, number],
+                recv_sems.at[index, number],
+                {"ctx": target},
+            )
+            copy.start()
+            copies.append(copy)
+        copy = pltpu.make_async_copy(
+            block_ref.at[ctx], out_ref.at[index, ctx], local_sems.at[index]
+        )
+        copy.start()
+        copies.append(copy)
+    for copy in copies:
+        copy.wait()
+
+
+def swap_blocks(blocks, collective_id):
+    arrays = len(blocks)
+    return pl.pallas_call(
+        functools.partial(swap_kernel, arrays),
+        out_shape=jax.ShapeDtypeStruct((arrays,) + blocks[0].shape, blocks[0].dtype),
+        in_specs=[pl.BlockSpec(memory_space=pltpu.VMEM)] * arrays,
+        out_specs=pl.BlockSpec(memory_space=pl.ANY),
+        scratch_shapes=[
+            pltpu.SemaphoreType.DMA((arrays,)),
+            pltpu.SemaphoreType.DMA((arrays, 3)),
+            pltpu.SemaphoreType.DMA((arrays, 3)),
+        ],
+        compiler_params=pltpu.CompilerParams(
+            collective_id=collective_id, has_side_effects=True, vmem_limit_bytes=VMEM_LIMIT
+        ),
+        name="swap_blocks",
+    )(*blocks)
+
+
+def dot(left, right):
+    return jnp.dot(left, right, preferred_element_type=jnp.float32)
+
+
+def turn(block):
+    return block.astype(jnp.float32).T.astype(block.dtype)
+
+
+def seen(prefix, row_block, key_block, rows, keys, values, fill):
+    if (key_block + 1) * keys <= row_block * rows + 1:
+        return values
+    key_pos = key_block * keys + lax.broadcasted_iota(jnp.int32, values.shape, 1)
+    row_pos = row_block * rows + lax.broadcasted_iota(jnp.int32, values.shape, 0)
+    allowed = key_pos < jnp.maximum(row_pos + 1, prefix)
+    return jnp.where(allowed, values, fill)
+
+
+def key_blocks(row_block, rows, keys, length):
+    farthest = max((row_block + 1) * rows, length // 2)
+    return range(-(-farthest // keys))
+
+
+def attend_kernel(rows, prefix_ref, blocks_ref, mixed_ref, log_ref, query_ref, value_ref):
+    places, keys = blocks_ref.shape[1], blocks_ref.shape[3]
+    length = places * keys
+    prefix = prefix_ref[0]
+    for block in range(places):
+        span = pl.ds(block * keys, keys)
+        query_ref[span, :] = turn(blocks_ref[0, block] * jnp.bfloat16(HEAD_DIM ** (-0.5)))
+        value_ref[span, :] = turn(blocks_ref[2, block])
+    for row_block in range(length // rows):
+        span = pl.ds(row_block * rows, rows)
+        queries = query_ref[span, :]
+        scores = []
+        for block in key_blocks(row_block, rows, keys, length):
+            scores.append(
+                seen(
+                    prefix, row_block, block, rows, keys, dot(queries, blocks_ref[1, block]), MASKED
+                )
+            )
+        row_max = functools.reduce(
+            jnp.maximum, [jnp.max(part, axis=1, keepdims=True) for part in scores]
+        )
+        row_sum = jnp.zeros_like(row_max)
+        mixed = jnp.zeros((rows, HEAD_DIM), jnp.float32)
+        for block, part in enumerate(scores):
+            exps = jnp.exp(part - row_max)
+            row_sum = row_sum + jnp.sum(exps, axis=1, keepdims=True)
+            mixed = mixed + dot(exps.astype(jnp.bfloat16), value_ref[pl.ds(block * keys, keys), :])
+        log_ref[0, span, :] = row_max + jnp.log(row_sum)
+        block, inside = divmod(row_block * rows, keys)
+        mixed_ref[block, :, pl.ds(inside, rows)] = (mixed / row_sum).T.astype(jnp.bfloat16)
+
+
+def attend(blocks, prefix):
+    _, places, features, keys = blocks.shape
+    heads = features // HEAD_DIM
+    length = places * keys
+    return pl.pallas_call(
+        functools.partial(attend_kernel, min(256, keys)),
+        grid=(heads,),
+        out_shape=(
+            jax.ShapeDtypeStruct((places, features, keys), jnp.bfloat16),
+            jax.ShapeDtypeStruct((heads, length, 1), jnp.float32),
+        ),
+        in_specs=[
+            pl.BlockSpec(memory_space=pltpu.SMEM),
+            pl.BlockSpec((3, places, HEAD_DIM, keys), lambda head: (0, 0, head, 0)),
+        ],
+        out_specs=(
+            pl.BlockSpec((places, HEAD_DIM, keys), lambda head: (0, head, 0)),
+            pl.BlockSpec((1, length, 1), lambda head: (head, 0, 0)),
+        ),
+        scratch_shapes=[
+            pltpu.VMEM((length, HEAD_DIM), jnp.bfloat16),
+            pltpu.VMEM((length, HEAD_DIM), jnp.bfloat16),
+        ],
+        compiler_params=pltpu.CompilerParams(vmem_limit_bytes=VMEM_LIMIT),
+        name="attend",
+    )(prefix, blocks)
+
+
+def turn_back(grads, cos_table, sine_table):
+    half = HEAD_DIM // 2
+    low, high = grads[:half], grads[half:]
+    return (
+        low * cos_table + high * sine_table,
+        high * cos_table - low * sine_table,
+    )
+
+
+def attend_back_kernel(
+    rows,
+    prefix_ref,
+    blocks_ref,
+    back_ref,
+    log_ref,
+    cos_ref,
+    sine_ref,
+    grads_ref,
+    query_ref,
+    key_ref,
+    attn_ref,
+    key_grad_ref,
+    value_grad_ref,
+):
+    places, keys = blocks_ref.shape[1], blocks_ref.shape[3]
+    length = places * keys
+    half = HEAD_DIM // 2
+    scale = HEAD_DIM ** (-0.5)
+    prefix = prefix_ref[0]
+    for block in range(places):
+        span = pl.ds(block * keys, keys)
+        query_ref[span, :] = turn(blocks_ref[0, block] * jnp.bfloat16(scale))
+        key_ref[span, :] = turn(blocks_ref[1, block])
+        attn_ref[span, :] = turn(back_ref[0, block])
+    key_grad_ref[...] = jnp.zeros_like(key_grad_ref)
+    value_grad_ref[...] = jnp.zeros_like(value_grad_ref)
+    for row_block in range(length // rows):
+        span = pl.ds(row_block * rows, rows)
+        home, inside = divmod(row_block * rows, keys)
+        lanes = pl.ds(inside, rows)
+        queries, attn_grad = query_ref[span, :], attn_ref[span, :]
+        queries_low = blocks_ref[0, home, :, lanes] * jnp.bfloat16(scale)
+        attn_low = back_ref[0, home, :, lanes]
+        total = log_ref[0, span, :]
+        reach = key_blocks(row_block, rows, keys, length)
+        weights, pulls = [], []
+        delta = jnp.zeros((rows, 1), jnp.float32)
+        for block in reach:
+            part = dot(queries, blocks_ref[1, block])
+            part = jnp.exp(seen(prefix, row_block, block, rows, keys, part, MASKED) - total)
+            pull = dot(attn_grad, blocks_ref[2, block])
+            delta = delta + jnp.sum(part * pull, axis=1, keepdims=True)
+            weights.append(part)
+            pulls.append(pull)
+        query_grad = jnp.zeros((rows, HEAD_DIM), jnp.float32)
+        for block in reach:
+            key_span = pl.ds(block * keys, keys)
+            score_grad = (weights[block] * (pulls[block] - delta)).astype(jnp.bfloat16)
+            query_grad = query_grad + dot(score_grad, key_ref[key_span, :])
+            key_grad_ref[:, key_span] += dot(queries_low, score_grad)
+            value_grad_ref[:, key_span] += dot(attn_low, weights[block].astype(jnp.bfloat16))
+        low, high = turn_back((query_grad * scale).T, cos_ref[:, span], sine_ref[:, span])
+        grads_ref[0, home, :half, lanes] = low.astype(jnp.bfloat16)
+        grads_ref[0, home, half:, lanes] = high.astype(jnp.bfloat16)
+    for block in range(places):
+        span = pl.ds(block * keys, keys)
+        low, high = turn_back(key_grad_ref[:, span], cos_ref[:, span], sine_ref[:, span])
+        grads_ref[1, block, :half] = low.astype(jnp.bfloat16)
+        grads_ref[1, block, half:] = high.astype(jnp.bfloat16)
+        grads_ref[2, block] = value_grad_ref[:, span].astype(jnp.bfloat16)
+
+
+def attend_back_heads(blocks, back, log_total, prefix, cos_table, sine_table):
+    _, places, features, keys = blocks.shape
+    heads = features // HEAD_DIM
+    length = places * keys
+    whole = pl.BlockSpec(memory_space=pltpu.VMEM)
+    return pl.pallas_call(
+        functools.partial(attend_back_kernel, min(256, keys)),
+        grid=(heads,),
+        out_shape=jax.ShapeDtypeStruct(blocks.shape, jnp.bfloat16),
+        in_specs=[
+            pl.BlockSpec(memory_space=pltpu.SMEM),
+            pl.BlockSpec((3, places, HEAD_DIM, keys), lambda head: (0, 0, head, 0)),
+            pl.BlockSpec((1, places, HEAD_DIM, keys), lambda head: (0, 0, head, 0)),
+            pl.BlockSpec((1, length, 1), lambda head: (head, 0, 0)),
+            whole,
+            whole,
+        ],
+        out_specs=pl.BlockSpec((3, places, HEAD_DIM, keys), lambda head: (0, 0, head, 0)),
+        scratch_shapes=[
+            pltpu.VMEM((length, HEAD_DIM), jnp.bfloat16),
+            pltpu.VMEM((length, HEAD_DIM), jnp.bfloat16),
+            pltpu.VMEM((length, HEAD_DIM), jnp.bfloat16),
+            pltpu.VMEM((HEAD_DIM, length), jnp.float32),
+            pltpu.VMEM((HEAD_DIM, length), jnp.float32),
+        ],
+        compiler_params=pltpu.CompilerParams(vmem_limit_bytes=VMEM_LIMIT),
+        name="attend_back",
+    )(prefix, blocks, back, log_total, cos_table, sine_table)
+
+
+def both_cores(part):
+    part = part.astype(jnp.bfloat16)
+    size = lax.axis_size("tp")
+    other = lax.ppermute(part, "tp", [(core, (core + 1) % size) for core in range(size)])
+    return part.astype(jnp.float32) + other.astype(jnp.float32)
+
+
+def matmul(spec, left, right):
+    return jnp.einsum(spec, left, right, preferred_element_type=jnp.float32)
+
+
+def half_tables(length):
+    half = HEAD_DIM // 2
+    frequency = jnp.exp(jnp.arange(half, dtype=jnp.float32) * (-2.0 * math.log(BASE) / HEAD_DIM))
+    angles = frequency[:, None] * jnp.arange(length, dtype=jnp.float32)[None, :]
+    return jnp.cos(angles), jnp.sin(angles)
+
+
+def norm_back(values, gain, grads):
+    scale = lax.rsqrt(jnp.mean(values * values, axis=-1, keepdims=True) + EPS)
+    pulled = grads * gain
+    inner = jnp.mean(values * pulled, axis=-1, keepdims=True)
+    gain_part = jnp.sum(grads * values * scale, axis=(0, 1))
+    return scale * pulled - values * (scale * scale * scale * inner), gain_part
+
+
+def gains_in(first, second):
+    both = jnp.stack([first.reshape(4, -1), second.reshape(4, -1)], axis=1)
+    both = jnp.pad(both, ((0, 0), (0, 14), (0, 128 - both.shape[2])))
+    return both.reshape(64, 128).astype(jnp.bfloat16)
+
+
+def gains_out(packed, which, quarter):
+    return packed.reshape(-1, 16, 128)[:, which, :quarter].reshape(-1)
+
+
+def heads_body(
+    layer_input,
+    output_cotangent,
+    prefix_len,
+    attn_gain,
+    mlp_gain,
+    query_weight,
+    key_weight,
+    value_weight,
+    out_weight,
+    gate_weight,
+    up_weight,
+    down_weight,
+):
+    block_len, seq_count, width = layer_input.shape
+    places = lax.axis_size("ctx")
+    ctx_index = lax.axis_index("ctx")
+    local = query_weight.shape[1]
+    features = seq_count * local // places
+    length = places * block_len
+    quarter = attn_gain.shape[0] // 4
+    low = jnp.bfloat16
+    shards = [
+        gains_in(attn_gain, mlp_gain),
+        query_weight.astype(low),
+        key_weight.astype(low),
+        value_weight.astype(low),
+        out_weight.T.astype(low),
+        gate_weight.astype(low),
+        up_weight.astype(low),
+        down_weight.T.astype(low),
+    ]
+    gains, full_query, full_key, full_value, full_out, full_gate, full_up, full_down = (
+        gather_shards(shards, 1)
+    )
+    attn_scale = gains_out(gains, 0, quarter).astype(jnp.float32)
+    mlp_scale = gains_out(gains, 1, quarter).astype(jnp.float32)
+    inputs = jnp.swapaxes(layer_input, 0, 1).astype(jnp.float32)
+    cotangent = jnp.swapaxes(output_cotangent, 0, 1)
+    cos_table, sine_table = half_tables(length)
+    own_cos = lax.dynamic_slice_in_dim(cos_table, ctx_index * block_len, block_len, 1)
+    own_sine = lax.dynamic_slice_in_dim(sine_table, ctx_index * block_len, block_len, 1)
+    prefix = lax.dynamic_slice_in_dim(prefix_len, ctx_index * seq_count // places, 1, 0)
+    normed_low = norm_rows(inputs, attn_scale).astype(low)
+    blocks_shape = (places, features, block_len)
+
+    def project(matrix, rotated):
+        product = matmul("bsd,de->bes", normed_low, matrix)
+        if rotated:
+            heads = product.reshape(seq_count, local // HEAD_DIM, 2, HEAD_DIM // 2, block_len)
+            first, second = heads[:, :, 0], heads[:, :, 1]
+            product = jnp.stack(
+                [first * own_cos - second * own_sine, second * own_cos + first * own_sine], axis=2
+            )
+        return product.astype(low).reshape(blocks_shape)
+
+    blocks = swap_blocks(
+        [project(full_query, True), project(full_key, True), project(full_value, False)], 2
+    )
+    mixed_heads, log_total = attend(blocks, prefix)
+    mixed_low = swap_blocks([mixed_heads], 3).reshape(seq_count, local, block_len)
+    hidden = inputs + both_cores(matmul("bes,de->bsd", mixed_low, full_out))
+    hnorm_low = norm_rows(hidden, mlp_scale).astype(low)
+    gate_out = matmul("bsd,df->bsf", hnorm_low, full_gate)
+    up_out = matmul("bsd,df->bsf", hnorm_low, full_up)
+    gate_sigmoid = jax.nn.sigmoid(gate_out)
+    silu = gate_out * gate_sigmoid
+    activated = (silu * up_out).astype(low)
+    layer_output = (hidden + both_cores(matmul("bsf,df->bsd", activated, full_down))).astype(low)
+    down_w_grad = matmul("bsd,bsf->df", cotangent, activated)
+    act_grad = matmul("bsd,df->bsf", cotangent, full_down)
+    gate_grad = (
+        act_grad * up_out * (gate_sigmoid * (1.0 + gate_out * (1.0 - gate_sigmoid)))
+    ).astype(low)
+    up_grad = (act_grad * silu).astype(low)
+    hnorm_part = matmul("bsf,df->bsd", gate_grad, full_gate) + matmul(
+        "bsf,df->bsd", up_grad, full_up
+    )
+    hnorm_grad = both_cores(hnorm_part)
+    gate_w_grad = matmul("bsd,bsf->df", hnorm_low, gate_grad)
+    up_w_grad = matmul("bsd,bsf->df", hnorm_low, up_grad)
+    hidden_back, mlp_gain_part = norm_back(hidden, mlp_scale, hnorm_grad)
+    hidden_grad = cotangent.astype(jnp.float32) + hidden_back
+    hidden_low = hidden_grad.astype(low)
+    attn_grad = matmul("bsd,de->bes", hidden_low, full_out).astype(low)
+    back = swap_blocks([attn_grad.reshape(blocks_shape)], 4)
+    out_w_grad = matmul("bsd,bes->de", hidden_low, mixed_low)
+    grads = attend_back_heads(blocks, back, log_total, prefix, cos_table, sine_table)
+    grads = swap_blocks([grads[0], grads[1], grads[2]], 5)
+    grads = grads.reshape(3, seq_count, local, block_len)
+    normed_part = (
+        matmul("bes,de->bsd", grads[0], full_query)
+        + matmul("bes,de->bsd", grads[1], full_key)
+        + matmul("bes,de->bsd", grads[2], full_value)
+    )
+    normed_grad = both_cores(normed_part)
+    input_back, attn_gain_part = norm_back(inputs, attn_scale, normed_grad)
+    input_grad = (hidden_grad + input_back).astype(low)
+    weight_grads = [
+        down_w_grad,
+        gate_w_grad,
+        up_w_grad,
+        out_w_grad,
+        matmul("bsd,bes->de", normed_low, grads[0]),
+        matmul("bsd,bes->de", normed_low, grads[1]),
+        matmul("bsd,bes->de", normed_low, grads[2]),
+    ]
+    count = lax.axis_size("fsdp")
+    gain_parts = jax.vmap(gains_in)(
+        attn_gain_part.reshape(count, -1), mlp_gain_part.reshape(count, -1)
+    ).reshape(-1, 128)
+    reduced = reduce_grads([gain_parts] + [grad.astype(low) for grad in weight_grads], 6)
+    gains, down, gate, up, out, query, key, value = [
+        total.astype(jnp.float32) for total in reduced
+    ]
+    return (
+        jnp.swapaxes(layer_output, 0, 1),
+        jnp.swapaxes(input_grad, 0, 1),
+        gains_out(gains, 0, quarter),
+        gains_out(gains, 1, quarter),
+        query,
+        key,
+        value,
+        out.T,
+        gate,
+        up,
+        down.T,
+    )
+
+
+def heads_divide(mesh, args):
+    block_rows = args[0].shape[0] // mesh.shape["ctx"]
+    seqs = args[0].shape[1] // mesh.shape["fsdp"]
+    heads = args[5].shape[1] // mesh.shape["tp"] // HEAD_DIM
+    places = mesh.shape["ctx"]
+    return (
+        places == 4
+        and mesh.shape["fsdp"] > 1
+        and places % seqs == 0
+        and heads % (places // seqs) == 0
+        and block_rows % 256 == 0
+    )
+
+
 def solution(mesh):
     placed = (
         P("ctx", "fsdp", None),
@@ -396,8 +1186,13 @@
         P("fsdp", "tp"),
         P("tp", "fsdp"),
     )
-    return jax.shard_map(
-        body,
+    def step(*args):
+        chosen = heads_body if heads_divide(mesh, args) else body
+        return spread_over(chosen)(*args)
+
+    def spread_over(chosen):
+      return jax.shard_map(
+        chosen,
         mesh=mesh,
         in_specs=placed,
         out_specs=(
@@ -415,3 +1210,5 @@
         ),
         check_vma=False,
     )
+
+    return step

time: 1120 us -> 402 us (0.36)
  waiting for transfers between devices: 622 us -> 0.01 us
  Pallas kernels: 0 us -> 289 us
  matrix products: 167 us -> 47 us
  blocking collectives: 96.7 us -> 0 us
  other arithmetic: 130 us -> 38.2 us
  between operations: 23.5 us -> 1.35 us
  local copies, waits for them, and re-layouts: 39.8 us -> 18.4 us
  starting transfers between devices: 20.4 us -> 0.74 us
  loops' own time: 13.2 us -> 0 us
    ppermute x14 -> x4, waiting for transfers between devices: 304 us -> 0.01 us  [both_cores(): lax.ppermute(part, 'tp', [(core, (core + 1) % size) for core in range(siz...]
    pallas_call x0 -> x8, Pallas kernels: none -> 289 us  [the longest x1 97.5 us: reduce_grads(): pl.pallas_call(functools.partial(reduce_kernel, chunks, len(grads)), out_...]
    reduce_scatter x7 -> x0, waiting for transfers between devices: 169 us -> none  [the longest x1 36.6 us: body(): lax.psum_scatter(gate_w_grad.astype(jnp.bfloat16), 'fsdp', scatter_dimens...]
    dot_general x49 -> x21, matrix products: 167 us -> 47 us  [matmul(): return jnp.einsum(spec, left, right, preferred_element_type=jnp.float32)]
    psum x4 -> x0, waiting for transfers between devices: 101 us -> none  [the longest x1 74.9 us: body(): lax.psum(shards[2].astype(jnp.bfloat16), 'ctx').astype(jnp.float32)]
    all_gather x4 -> x0, blocking collectives: 63.4 us -> none  [the longest x1 16.6 us: body(): lax.all_gather(key_weight.astype(jnp.bfloat16), 'fsdp', axis=0, tiled=True)]
    convert_element_type x33 -> x14, other arithmetic: 65.7 us -> 14.2 us  [the longest x5 6.86 us: heads_body(): total.astype(jnp.float32)]
    all_gather x3 -> x0, waiting for transfers between devices: 47.3 us -> none  [the longest x1 31.8 us: body(): lax.all_gather(up_weight.astype(jnp.bfloat16), 'fsdp', axis=0, tiled=True)]
  transfers between devices with their start and end apart: 28 -> 4, of which waited for: 22 -> 0; matrix products, arithmetic and copies ran while one was open for 16% -> 7% of each run, Pallas kernels for 0% -> 0%
where the time goes in v1:
time: 402 us; the launch traced here: 395 us
  Pallas kernels  289 us (72%)
  matrix products  47 us (12%)
  other arithmetic  38.2 us (10%)
  local copies, waits for them, and re-layouts  18.4 us (5%)
    pallas_call x1, Pallas kernels, reduce_grads(): pl.pallas_call(functools.partial(reduce_kernel, chunks, len(grads)), out_...  97.5 us
    pallas_call x4, Pallas kernels, swap_blocks(): pl.pallas_call(functools.partial(swap_kernel, arrays), out_shape=jax.Shap...  84.6 us
    pallas_call x1, Pallas kernels, gather_shards(): pl.pallas_call(functools.partial(gather_kernel, chunks, len(shards)), out...  57.9 us
    dot_general x21, matrix products, matmul(): return jnp.einsum(spec, left, right, preferred_element_type=jnp.float32)  47 us
    pallas_call x1, Pallas kernels, attend_back_heads(): pl.pallas_call(functools.partial(attend_back_kernel, min(256, keys)), gri...  30 us
    pallas_call x1, Pallas kernels, attend(): pl.pallas_call(functools.partial(attend_kernel, min(256, keys)), grid=(he...  19.3 us
    unnamed x70, local copies, waits for them, and re-layouts  9 us
  transfers between devices with their start and end apart: 4, of which 0 were waited for; matrix products, arithmetic and copies ran while one was open for 7% of the time, Pallas kernels for 0%

profile of v1, /device:TPU:0, one launch (start us, length us, event | category | flops | bytes accessed | tf_op | source)
XLA Modules:
  0.0 395.1 jit_solution(9822529677888032105)
XLA Ops:
  2.4 1.9 fusion.4
  4.3 1.7 convert_element_type.191.refs_1_
  10.5 1.8 fusion.50
  12.9 57.9 %gather_shards.1 = (bf16[256,128]{1,0:T(8,128)(2,1)}, bf16[768,384]{1,0:T(8,128)(2,1)}, bf16[768,384]{1,0:T(8,128)(2,1)}, bf16[768,384]{1,0:T(8,128)(2,1)}, bf16...) custom-call(bf16[64,128]{1,0:T(8,128)(2,1)} %bitcast.206, ...), custom_call_target="tpu_custom_call" | custom-call | tf_op jit(solution)/shard_map/gather_shards/pallas_call | solution.py:593
  71.7 3.0 convolution_convert_fusion.3
  74.7 1.0 fusion.43
  75.8 2.1 fusion.47
  79.4 1.9 subtract_convert_fusion
  83.2 28.8 %swap_blocks.4.blocks_ref = bf16[3,4,192,512]{3,2,1,0:T(8,128)(2,1)} custom-call(bf16[4,192,512]{2,1,0:T(8,128)(2,1)} %bitcast.187, bf16[4,192,512]{2,1,0:T(8,128)(2,1)} %bitcast.186, bf16[4,192,512]{2,1,0:T(8,128)(2,1)} %bitcast.201), custom_call_target="tpu_custom_call" | custom-call | tf_op jit(solution)/shard_map/swap_blocks/pallas_call | solution.py:793
  112.0 19.3 %attend.1 = (bf16[4,192,512]{2,1,0:T(8,128)(2,1)}, f32[3,2048,1]{2,1,0:T(8,128)}) custom-call(s32[1]{0:T(128)} %dynamic_slice.9.prefix_ref, bf16[3,4,192,512]{3,2,1,0:T(8,128)(2,1)} %swap_blocks.4.blocks_ref), custom_call_target="tpu_custom_call" | custom-call | tf_op jit(solution)/shard_map/attend/pallas_call | solution.py:868
  131.3 12.2 %swap_blocks.5 = bf16[1,4,192,512]{3,2,1,0:T(8,128)(2,1)} custom-call(bf16[4,192,512]{2,1,0:T(8,128)(2,1)} %get-tuple-element.33.refs_0_), custom_call_target="tpu_custom_call" | custom-call | tf_op jit(solution)/shard_map/swap_blocks/pallas_call | solution.py:793
  143.5 2.3 convolution_convert_fusion
  145.9 3.8 fusion.18
  149.7 2.1 multiply_reduce_fusion.2
  152.2 1.1 copy-done.28
  153.2 1.8 fusion.23
  155.0 4.2 %fusion.2 = (bf16[2,512,1024]{2,1,0:T(8,128)(2,1)S(1)}, bf16[2,512,1024]{2,1,0:T(8,128)(2,1)S(1)}, bf16[2,512,1024]{2,1,0:T(8,128)(2,1)S(1)}) fusion(f32[1024,2,512]{0,2,1:T(8,128)S(1)} %fusion.18, f32[2,512,1024]{2,1,0:T(8,128)S(1)} %fusion.23, bf16[2,512,768]{2,1,0:T(8,128)(2,1)S(1)} %multiply_convert_fusion.1, bf16[768,1024]{1,0:T(8,128)(2,1)S(1)} %copy-done.29), kind=kOutput, calls=%fused_computation.4 | convolution fusion | flops 1626341376 | bytes 17825792 | tf_op jit(solution)/shard_map/bsd,df->bsf/dot_general | solution.py:1002
  159.3 1.8 fusion.25
  161.1 1.8 add_convert_fusion.1
  163.5 1.8 convolution_convert_fusion.1
  165.5 3.1 bitcast_convert_fusion
  168.6 3.0 bitcast_convert_fusion.1
  171.6 1.2 multiply_reduce_fusion
  173.0 2.3 subtract_add_fusion
  175.3 1.7 convolution_convert_fusion.2
  177.0 13.7 %swap_blocks.6.back_ref = bf16[1,4,192,512]{3,2,1,0:T(8,128)(2,1)} custom-call(bf16[4,192,512]{2,1,0:T(8,128)(2,1)} %bitcast.194), custom_call_target="tpu_custom_call" | custom-call | tf_op jit(solution)/shard_map/swap_blocks/pallas_call | solution.py:793
  190.7 30.0 %attend_back.1 = bf16[3,4,192,512]{3,2,1,0:T(8,128)(2,1)} custom-call(s32[1]{0:T(128)} %dynamic_slice.9.prefix_ref, bf16[3,4,192,512]{3,2,1,0:T(8,128)(2,1)} %swap_blocks.4.blocks_ref, bf16[1,4,192,512]{3,2,1,0:T(8,128)(2,1)} %swap_blocks.6.back_ref, f32[3,2048,1]{2,1,0:T(8,128)} %get-tuple-element.38.log_ref, f32[32,2048]{1,0:T(8,128)} %copy-done.11, ...), custom_call_target="tpu_custom_call" | custom-call | tf_op jit(solution)/shard_map/attend_back/pallas_call | solution.py:969
  220.8 3.1 slice_bitcast_fusion
  223.8 29.9 %swap_blocks.7 = bf16[3,4,192,512]{3,2,1,0:T(8,128)(2,1)} custom-call(bf16[4,192,512]{2,1,0:T(8,128)(2,1)} %get-tuple-element.89.refs_0_, bf16[4,192,512]{2,1,0:T(8,128)(2,1)} %get-tuple-element.88.refs_1_, bf16[4,192,512]{2,1,0:T(8,128)(2,1)} %get-tuple-element.87.refs_2_), custom_call_target="tpu_custom_call" | custom-call | tf_op jit(solution)/shard_map/swap_blocks/pallas_call | solution.py:793
  253.7 1.9 fusion.61
  255.6 1.0 fusion.45
  257.1 1.0 fusion.41
  258.2 2.2 add_convert_fusion
  260.4 3.0 bitcast_convert_fusion.2
  263.5 4.3 %copy.65 = bf16[512,2,768]{2,1,0:T(2,128)(2,1)} copy(bf16[512,2,768]{2,0,1:T(8,128)(2,1)} %get-tuple-element.83) | data formatting | bytes 3145728
  267.9 2.1 fusion.31
  270.0 2.1 fusion.32
  272.1 2.1 fusion.30
  274.2 1.9 fusion.29
  276.1 3.6 fusion.12
  279.7 2.4 fusion.16
  282.1 2.8 copy.66
  285.7 97.5 %reduce_grads.1 = (bf16[64,128]{1,0:T(8,128)(2,1)}, bf16[192,1024]{1,0:T(8,128)(2,1)}, bf16[192,1024]{1,0:T(8,128)(2,1)}, bf16[192,1024]{1,0:T(8,128)(2,1)}, bf1...) custom-call(bf16[4,64,128]{2,1,0:T(8,128)(2,1)} %bitcast.205, ...), custom_call_target="tpu_custom_call" | custom-call | tf_op jit(solution)/shard_map/reduce_grads/pallas_call | solution.py:751
  385.4 1.6 convert_element_type.240
  387.0 1.6 convert_element_type.241
  388.7 1.6 convert_element_type.242
  390.3 1.6 convert_bitcast_fusion.2
  391.9 1.0 convert_element_type.243
  (110 shorter events, 18.0 us)
Async XLA Ops:
  0.6 5.4 %copy-start.24 = (f32[192,384]{1,0:T(8,128)S(1)}, f32[192,384]{1,0:T(8,128)}, u32[]{:S(2)}) copy-start(f32[192,384]{1,0:T(8,128)} %param.18) | copy-start | bytes 884740
  0.7 6.0 %copy-start.25 = (f32[192,384]{1,0:T(8,128)S(1)}, f32[192,384]{1,0:T(8,128)}, u32[]{:S(2)}) copy-start(f32[192,384]{1,0:T(8,128)} %param.19) | copy-start | bytes 884740
  0.7 6.7 %copy-start.26 = (f32[384,192]{0,1:T(8,128)S(1)}, f32[384,192]{0,1:T(8,128)}, u32[]{:S(2)}) copy-start(f32[384,192]{0,1:T(8,128)} %param.20) | copy-start | bytes 884740
  0.7 7.4 %copy-start.12 = (f32[192,1024]{1,0:T(8,128)S(1)}, f32[192,1024]{1,0:T(8,128)}, u32[]{:S(2)}) copy-start(f32[192,1024]{1,0:T(8,128)} %param.21) | copy-start | bytes 2359300
  2.4 6.5 %copy-start.13 = (f32[192,1024]{1,0:T(8,128)S(1)}, f32[192,1024]{1,0:T(8,128)}, u32[]{:S(2)}) copy-start(f32[192,1024]{1,0:T(8,128)} %param.22) | copy-start | bytes 2359300
  4.3 5.4 %copy-start.14 = (f32[1024,192]{0,1:T(8,128)S(1)}, f32[1024,192]{0,1:T(8,128)}, u32[]{:S(2)}) copy-start(f32[1024,192]{0,1:T(8,128)} %param.23) | copy-start | bytes 2359300
  8.9 62.9 %copy-start = (bf16[512,2,768]{2,1,0:T(2,128)(2,1)S(1)}, bf16[512,2,768]{2,1,0:T(2,128)(2,1)}, u32[]{:S(2)}) copy-start(bf16[512,2,768]{2,1,0:T(2,128)(2,1)} %param.12) | copy-start | bytes 4718596
  12.2 66.3 %copy-start.11 = (f32[32,2048]{1,0:T(8,128)}, f32[32,2048]{1,0:T(8,128)S(1)}, u32[]{:S(2)}) copy-start(f32[32,2048]{1,0:T(8,128)S(1)} %get-tuple-element.96.cos_ref) | copy-start | bytes 786436
  71.7 3.0 copy-start.16
  74.7 1.1 copy-start.18
  75.8 2.2 copy-start.30
  145.8 3.9 collective-permute-start
  151.8 1.4 copy-start.28
  153.2 1.8 copy-start.29
  159.3 4.3 %copy-start.31 = (bf16[2,512,1024]{2,1,0:T(8,128)(2,1)}, bf16[2,512,1024]{2,1,0:T(8,128)(2,1)S(1)}, u32[]{:S(2)}) copy-start(bf16[2,512,1024]{2,1,0:T(8,128)(2,1)S(1)} %get-tuple-element.81) | copy-start | bytes 6291460
  161.1 2.4 copy-start.27
  163.0 8.6 %collective-permute-start.2 = (bf16[2,512,768]{2,1,0:T(8,128)(2,1)S(1)}, bf16[2,512,768]{2,1,0:T(8,128)(2,1)S(1)}, u32[]{:S(2)}, u32[]{:S(2)}) collective-permute-start(bf16[2,512,768]{2,1,0:T(8,128)(2,1)S(1)} %add_convert_fusion.1), channel_id=1, source_target_pairs={{0,1},{1,0},{2,3},{3,2},{4,5},{5,4},{6,7},{7,6},{8,9},{9,8},{10,11... | collective-permute-start | bytes 4718600 | tf_op jit(solution)/shard_map/ppermute | solution.py:997
  165.4 7.5 %collective-permute-start.1 = (bf16[2,512,768]{2,1,0:T(8,128)(2,1)S(1)}, bf16[2,512,768]{2,1,0:T(8,128)(2,1)S(1)}, u32[]{:S(2)}, u32[]{:S(2)}) collective-permute-start(bf16[2,512,768]{2,1,0:T(8,128)(2,1)S(1)} %convolution_convert_fusion.1), channel_id=1, source_target_pairs={{0,1},{1,0},{2,3},{3,2},{4,5},{5,4},{6,7},{7,6},{8,9},{9,8},{10,11... | collective-permute-start | bytes 4718600 | tf_op jit(solution)/shard_map/ppermute | solution.py:997
  171.6 1.4 copy-start.9
  172.8 2.4 copy-start.20
  253.7 1.9 copy-start.19
  255.6 1.1 copy-start.4
  255.6 1.1 copy-start.6
  255.6 2.6 copy-start.2
  255.6 1.5 copy-start.17
  257.1 1.1 copy-start.15
  258.2 2.2 copy-start.10
  258.2 2.2 copy-start.32
  260.4 15.7 %collective-permute-start.3 = (bf16[2,512,768]{2,1,0:T(8,128)(2,1)}, bf16[2,512,768]{2,1,0:T(8,128)(2,1)}, u32[]{:S(2)}, u32[]{:S(2)}) collective-permute-start(bf16[2,512,768]{2,1,0:T(8,128)(2,1)} %add_convert_fusion), channel_id=1, source_target_pairs={{0,1},{1,0},{2,3},{3,2},{4,5},{5,4},{6,7},{7,6},{8,9},{9,8},{10,11... | collective-permute-start | bytes 4718600 | tf_op jit(solution)/shard_map/ppermute | solution.py:997
  263.5 4.3 %copy-start.1 = (bf16[512,2,768]{2,1,0:T(2,128)(2,1)S(1)}, bf16[512,2,768]{2,1,0:T(2,128)(2,1)}, u32[]{:S(2)}) copy-start(bf16[512,2,768]{2,1,0:T(2,128)(2,1)} %param.12) | copy-start | bytes 4718596
  263.5 4.3 %copy-start.7 = (bf16[1,4,192,512]{3,2,1,0:T(8,128)(2,1)S(1)}, bf16[1,4,192,512]{3,2,1,0:T(8,128)(2,1)}, u32[]{:S(2)}) copy-start(bf16[1,4,192,512]{3,2,1,0:T(8,128)(2,1)} %copy-done.6) | copy-start | bytes 2359300
  267.9 2.1 copy-start.3
  270.0 2.1 copy-start.5
  272.1 2.1 copy-start.8
  383.2 8.7 %copy-start.23 = (bf16[192,1024]{1,0:T(8,128)(2,1)S(1)}, bf16[192,1024]{1,0:T(8,128)(2,1)}, u32[]{:S(2)}) copy-start(bf16[192,1024]{1,0:T(8,128)(2,1)} %get-tuple-element.44) | copy-start | bytes 1179652
  383.2 9.7 %copy-start.22 = (bf16[192,1024]{1,0:T(8,128)(2,1)S(1)}, bf16[192,1024]{1,0:T(8,128)(2,1)}, u32[]{:S(2)}) copy-start(bf16[192,1024]{1,0:T(8,128)(2,1)} %get-tuple-element.45) | copy-start | bytes 1179652
  383.2 10.6 %copy-start.21 = (bf16[192,1024]{1,0:T(8,128)(2,1)S(1)}, bf16[192,1024]{1,0:T(8,128)(2,1)}, u32[]{:S(2)}) copy-start(bf16[192,1024]{1,0:T(8,128)(2,1)} %get-tuple-element.46) | copy-start | bytes 1179652

commit v2 on v1

--- a/solution.py
+++ b/solution.py
@@ -386,6 +386,7 @@
 
 MESH = pl.DeviceIdType.MESH
 VMEM_LIMIT = 60 << 20
+LINE = 2
 
 
 def place():
@@ -417,7 +418,7 @@
     )
 
 
-def column_chunks(shapes, widest):
+def column_chunks(shapes, widest, paths=2):
     chunks = []
     for index, (rows, columns) in enumerate(shapes):
         count = -(-columns // widest)
@@ -425,7 +426,7 @@
             count += 1
         width = columns // count
         chunks += [(index, rows // 4, part * width, width) for part in range(count)]
-    return [chunk + (number % 2,) for number, chunk in enumerate(chunks)]
+    return [chunk + (number % paths,) for number, chunk in enumerate(chunks)]
 
 
 def gather_steps(chunks, shard_refs, full_refs, local_sem, send_sems, recv_sems):
@@ -433,7 +434,9 @@
     last = lax.axis_size("fsdp") - 1
 
     def region(chunk, shard, quarter):
-        index, rows, low, width, _ = chunk
+        index, rows, low, width, path = chunk
+        if path == LINE:
+            return full_refs[index].at[rows_at(shard, 4 * rows), pl.ds(low, width)]
         return full_refs[index].at[rows_at(shard * 4 + quarter, rows), pl.ds(low, width)]
 
     def pass_on(number, shard, quarter, kind, device, source=None):
@@ -447,7 +450,9 @@
         )
 
     def own_source(number):
-        index, rows, low, width, _ = chunks[number]
+        index, rows, low, width, path = chunks[number]
+        if path == LINE:
+            return shard_refs[index].at[:, pl.ds(low, width)]
         return shard_refs[index].at[rows_at(ctx, rows), pl.ds(low, width)]
 
     def arrived(number, shard, quarter):
@@ -497,12 +502,16 @@
                 def _():
                     pass_on(number, shard, ctx, 1, down).start()
 
-            pass_on(number, shard, ctx, 2, to_x).start()
-            pass_on(number, shard, ctx, 3, to_y).start()
+            if chunks[number][-1] != LINE:
+                pass_on(number, shard, ctx, 2, to_x).start()
+                pass_on(number, shard, ctx, 3, to_y).start()
 
         each(steps, act)
 
     def to_corner(number, steps):
+        if chunks[number][-1] == LINE:
+            return
+
         def act(shard, sign):
             if chunks[number][-1] == 0:
                 arrived(number, shard, along_x)
@@ -518,16 +527,18 @@
             for number in count:
 
                 def act(shard, sign, number=number):
-                    arrived(number, shard, along_y if chunks[number][-1] == 0 else along_x)
-                    arrived(number, shard, across)
+                    if chunks[number][-1] != LINE:
+                        arrived(number, shard, along_y if chunks[number][-1] == 0 else along_x)
+                        arrived(number, shard, across)
                     forward = fsdp < last if sign < 0 else fsdp > 0
 
                     @pl.when(forward)
                     def _():
                         pass_on(number, shard, ctx, 0 if sign < 0 else 1, up).wait_send()
 
-                    for kind in (2, 3, 4):
-                        pass_on(number, shard, ctx, kind, to_x).wait_send()
+                    if chunks[number][-1] != LINE:
+                        for kind in (2, 3, 4):
+                            pass_on(number, shard, ctx, kind, to_x).wait_send()
 
                 each(steps, act)
         for number in count:
@@ -606,16 +617,13 @@
     )(*shards)
 
 
-def reduce_kernel(chunks, arrays, *refs):
-    full_refs, out_refs = refs[:arrays], refs[arrays : 2 * arrays]
-    rest = refs[2 * arrays :]
+def reduce_steps(chunks, full_refs, out_refs, rest):
     count = len(chunks)
     buffers = [rest[6 * number : 6 * number + 6] for number in range(count)]
     load_sems, send_sems, recv_sems = rest[6 * count :]
     fsdp, ctx, along_x, along_y, across = place()
     size = lax.axis_size("fsdp")
     others = [{"fsdp": lax.rem(fsdp + step, size)} for step in range(1, size)]
-    greet([{"ctx": along_x}, {"ctx": along_y}] + others)
 
     def quarter_of(number, quarter):
         index, rows, low, width, _ = chunks[number]
@@ -723,14 +731,47 @@
             for kind in range(3):
                 spread(number, ctx, kind, first).wait_send()
 
-    for number in range(count):
+    return stage
+
+
+def reduce_order(count, lag):
+    return [
+        (number, at)
+        for tick in range(count + 4 * lag)
+        for at in range(5, 0, -1)
+        for number in (tick - (at - 1) * lag,)
+        if 0 <= number < count
+    ]
+
+
+def close_by():
+    fsdp, ctx, along_x, along_y, across = place()
+    size = lax.axis_size("fsdp")
+    return [{"ctx": along_x}, {"ctx": along_y}, {"ctx": across}] + [
+        {"fsdp": lax.rem(fsdp + step, size)} for step in range(1, size)
+    ]
+
+
+def reduce_kernel(chunks, arrays, *refs):
+    greet(close_by())
+    stage = reduce_steps(chunks, refs[:arrays], refs[arrays : 2 * arrays], refs[2 * arrays :])
+    for number in range(len(chunks)):
         stage(number, 0)
-    lag = 2
-    for tick in range(count + 4 * lag):
-        for at in range(5, 0, -1):
-            number = tick - (at - 1) * lag
-            if 0 <= number < count:
-                stage(number, at)
+    for number, at in reduce_order(len(chunks), 2):
+        stage(number, at)
+
+
+def reduce_scratch(chunks, size):
+    scratch = []
+    for _, rows, _, width, _ in chunks:
+        block = (size, rows, width)
+        for shape in ((2,) + block, (2,) + block, block, block, block, (size - 1, rows, width)):
+            scratch.append(pltpu.VMEM(shape, jnp.bfloat16))
+    return scratch + [
+        pltpu.SemaphoreType.DMA((len(chunks), 2)),
+        pltpu.SemaphoreType.DMA((len(chunks), size + 5)),
+        pltpu.SemaphoreType.DMA((len(chunks), size + 5)),
+    ]
 
 
 def reduce_grads(grads, collective_id):
@@ -738,22 +779,12 @@
     shapes = [(grad.shape[0] // size, grad.shape[1]) for grad in grads]
     chunks = column_chunks(shapes, 512)
     anywhere = pl.BlockSpec(memory_space=pl.ANY)
-    scratch = []
-    for _, rows, _, width, _ in chunks:
-        block = (size, rows, width)
-        for shape in ((2,) + block, (2,) + block, block, block, block, (size - 1, rows, width)):
-            scratch.append(pltpu.VMEM(shape, jnp.bfloat16))
-    scratch += [
-        pltpu.SemaphoreType.DMA((len(chunks), 2)),
-        pltpu.SemaphoreType.DMA((len(chunks), size + 5)),
-        pltpu.SemaphoreType.DMA((len(chunks), size + 5)),
-    ]
     return pl.pallas_call(
         functools.partial(reduce_kernel, chunks, len(grads)),
         out_shape=[jax.ShapeDtypeStruct(shape, jnp.bfloat16) for shape in shapes],
         in_specs=[anywhere] * len(grads),
         out_specs=[pl.BlockSpec(memory_space=pltpu.VMEM)] * len(grads),
-        scratch_shapes=scratch,
+        scratch_shapes=reduce_scratch(chunks, size),
         compiler_params=pltpu.CompilerParams(
             collective_id=collective_id, has_side_effects=True, vmem_limit_bytes=VMEM_LIMIT
         ),
@@ -761,50 +792,81 @@
     )(*[grad.reshape(size, shape[0], shape[1]) for grad, shape in zip(grads, shapes)])
 
 
-def swap_kernel(arrays, *refs):
-    block_refs, out_ref = refs[:arrays], refs[arrays]
-    local_sems, send_sems, recv_sems = refs[arrays + 1 :]
+def head_rows(head):
+    return pl.ds(pl.multiple_of(head * HEAD_DIM, HEAD_DIM), HEAD_DIM)
+
+
+def swap_steps(sources, landings, local_sems, send_sems, recv_sems):
     fsdp, ctx, along_x, along_y, across = place()
     targets = (across, along_x, along_y)
-    greet([{"ctx": target} for target in targets])
-    copies = []
-    for index, block_ref in enumerate(block_refs):
-        for number, target in enumerate(targets):
-            copy = send(
-                block_ref.at[target],
-                out_ref.at[index, ctx],
-                send_sems.at[index, number],
-                recv_sems.at[index, number],
-                {"ctx": target},
-            )
+
+    def copies(head, local=True):
+        rows = head_rows(head)
+        made = []
+        for index, (source, landing) in enumerate(zip(sources, landings)):
+            for number, target in enumerate(targets):
+                made.append(
+                    send(
+                        source.at[target, rows],
+                        landing.at[ctx, rows],
+                        send_sems.at[head, index, number],
+                        recv_sems.at[head, index, number],
+                        {"ctx": target},
+                    )
+                )
+            if local:
+                made.append(
+                    pltpu.make_async_copy(
+                        source.at[ctx, rows], landing.at[ctx, rows], local_sems.at[head, index]
+                    )
+                )
+        return made
+
+    def begin(head):
+        for copy in copies(head):
             copy.start()
-            copies.append(copy)
-        copy = pltpu.make_async_copy(
-            block_ref.at[ctx], out_ref.at[index, ctx], local_sems.at[index]
-        )
-        copy.start()
-        copies.append(copy)
-    for copy in copies:
-        copy.wait()
-
-
-def swap_blocks(blocks, collective_id):
-    arrays = len(blocks)
-    return pl.pallas_call(
-        functools.partial(swap_kernel, arrays),
-        out_shape=jax.ShapeDtypeStruct((arrays,) + blocks[0].shape, blocks[0].dtype),
-        in_specs=[pl.BlockSpec(memory_space=pltpu.VMEM)] * arrays,
-        out_specs=pl.BlockSpec(memory_space=pl.ANY),
-        scratch_shapes=[
-            pltpu.SemaphoreType.DMA((arrays,)),
-            pltpu.SemaphoreType.DMA((arrays, 3)),
-            pltpu.SemaphoreType.DMA((arrays, 3)),
-        ],
-        compiler_params=pltpu.CompilerParams(
-            collective_id=collective_id, has_side_effects=True, vmem_limit_bytes=VMEM_LIMIT
-        ),
-        name="swap_blocks",
-    )(*blocks)
+
+    def landed(head):
+        for number, copy in enumerate(copies(head)):
+            if number % 4 == 3:
+                copy.wait()
+            else:
+                copy.wait_recv()
+
+    def sent(head):
+        for copy in copies(head, local=False):
+            copy.wait_send()
+
+    return begin, landed, sent
+
+
+def swap_scratch(heads, arrays):
+    return [
+        pltpu.SemaphoreType.DMA((heads, arrays)),
+        pltpu.SemaphoreType.DMA((heads, arrays, 3)),
+        pltpu.SemaphoreType.DMA((heads, arrays, 3)),
+    ]
+
+
+def beside(head, slot, events):
+    for at in sorted({event[0] for event in events if event[1] == slot}):
+
+        @pl.when(head == at)
+        def _(at=at):
+            for planned, place_in, act in events:
+                if planned == at and place_in == slot:
+                    act()
+
+
+def spaced(acts, slots, heads, first, gap):
+    planned, left = [], []
+    for number, act in enumerate(acts):
+        at = first + int(number * gap)
+        if at < slots * heads:
+            planned.append((at // slots, at % slots, act))
+        else:
+            left.append(act)
+    return planned, left
 
 
 def dot(left, right):
@@ -829,64 +891,119 @@
     return range(-(-farthest // keys))
 
 
-def attend_kernel(rows, prefix_ref, blocks_ref, mixed_ref, log_ref, query_ref, value_ref):
-    places, keys = blocks_ref.shape[1], blocks_ref.shape[3]
-    length = places * keys
-    prefix = prefix_ref[0]
-    for block in range(places):
-        span = pl.ds(block * keys, keys)
-        query_ref[span, :] = turn(blocks_ref[0, block] * jnp.bfloat16(HEAD_DIM ** (-0.5)))
-        value_ref[span, :] = turn(blocks_ref[2, block])
-    for row_block in range(length // rows):
-        span = pl.ds(row_block * rows, rows)
-        queries = query_ref[span, :]
-        scores = []
-        for block in key_blocks(row_block, rows, keys, length):
-            scores.append(
-                seen(
-                    prefix, row_block, block, rows, keys, dot(queries, blocks_ref[1, block]), MASKED
-                )
-            )
-        row_max = functools.reduce(
-            jnp.maximum, [jnp.max(part, axis=1, keepdims=True) for part in scores]
-        )
-        row_sum = jnp.zeros_like(row_max)
-        mixed = jnp.zeros((rows, HEAD_DIM), jnp.float32)
-        for block, part in enumerate(scores):
-            exps = jnp.exp(part - row_max)
-            row_sum = row_sum + jnp.sum(exps, axis=1, keepdims=True)
-            mixed = mixed + dot(exps.astype(jnp.bfloat16), value_ref[pl.ds(block * keys, keys), :])
-        log_ref[0, span, :] = row_max + jnp.log(row_sum)
-        block, inside = divmod(row_block * rows, keys)
-        mixed_ref[block, :, pl.ds(inside, rows)] = (mixed / row_sum).T.astype(jnp.bfloat16)
-
-
-def attend(blocks, prefix):
-    _, places, features, keys = blocks.shape
+def attend_kernel(rows, chunks, arrays, *refs):
+    prefix_ref, query_in, key_in, value_in = refs[:4]
+    shard_refs, refs = refs[4 : 4 + arrays], refs[4 + arrays :]
+    query_blocks, key_blocks_ref, value_blocks, mixed_out, log_ref = refs[:5]
+    full_refs, refs = refs[5 : 5 + arrays], refs[5 + arrays :]
+    mixed_ref, query_ref, value_ref = refs[:3]
+    fsdp, ctx, along_x, along_y, across = place()
+    places, features, keys = query_in.shape
     heads = features // HEAD_DIM
     length = places * keys
+    greet(close_by())
+    begin, landed, sent = swap_steps(
+        (query_in, key_in, value_in), (query_blocks, key_blocks_ref, value_blocks), *refs[3:6]
+    )
+    begin_back, landed_back, sent_back = swap_steps((mixed_ref,), (mixed_out,), *refs[6:9])
+    begin_gather, from_line, to_corner, finish = gather_steps(
+        chunks, shard_refs, full_refs, *refs[9:12]
+    )
+    for head in range(heads):
+        begin(head)
+    begin_gather()
+    last = lax.axis_size("fsdp") - 1
+    acts = []
+    for steps in range(1, last + 2):
+        for number in range(len(chunks)):
+            if steps <= last:
+                acts.append(functools.partial(from_line, number, steps))
+            if steps > 1:
+                acts.append(functools.partial(to_corner, number, steps - 1))
+    slots = length // rows
+    planned, left = spaced(acts, slots, heads, 1, slots * heads / len(acts))
+    prefix = prefix_ref[0]
+
+    @pl.loop(0, heads)
+    def _(head):
+        landed(head)
+        inside_rows = head_rows(head)
+        for block in range(places):
+            span = pl.ds(block * keys, keys)
+            query_ref[span, :] = turn(
+                query_blocks[block, inside_rows] * jnp.bfloat16(HEAD_DIM ** (-0.5))
+            )
+            value_ref[span, :] = turn(value_blocks[block, inside_rows])
+        for row_block in range(length // rows):
+            span = pl.ds(row_block * rows, rows)
+            queries = query_ref[span, :]
+            scores = []
+            for block in key_blocks(row_block, rows, keys, length):
+                part = dot(queries, key_blocks_ref[block, inside_rows])
+                scores.append(seen(prefix, row_block, block, rows, keys, part, MASKED))
+            row_max = functools.reduce(
+                jnp.maximum, [jnp.max(part, axis=1, keepdims=True) for part in scores]
+            )
+            row_sum = jnp.zeros_like(row_max)
+            mixed = jnp.zeros((rows, HEAD_DIM), jnp.float32)
+            for block, part in enumerate(scores):
+                exps = jnp.exp(part - row_max)
+                row_sum = row_sum + jnp.sum(exps, axis=1, keepdims=True)
+                mixed = mixed + dot(
+                    exps.astype(jnp.bfloat16), value_ref[pl.ds(block * keys, keys), :]
+                )
+            log_ref[head, span, :] = row_max + jnp.log(row_sum)
+            block, inside = divmod(row_block * rows, keys)
+            mixed_ref[block, inside_rows, pl.ds(inside, rows)] = (mixed / row_sum).T.astype(
+                jnp.bfloat16
+            )
+            beside(head, row_block, planned)
+        begin_back(head)
+
+    for act in left:
+        act()
+    finish()
+    for head in range(heads):
+        landed_back(head)
+        sent(head)
+        sent_back(head)
+
+
+def attend(query, key, value, shards, prefix, collective_id):
+    places, features, keys = query.shape
+    heads = features // HEAD_DIM
+    length = places * keys
+    size = lax.axis_size("fsdp")
+    chunks = column_chunks([shard.shape for shard in shards], 512)
+    chunks = [
+        chunk[:-1] + (LINE if number % 2 else number // 2 % 2,)
+        for number, chunk in enumerate(chunks)
+    ]
+    held = pl.BlockSpec(memory_space=pltpu.VMEM)
+    anywhere = pl.BlockSpec(memory_space=pl.ANY)
     return pl.pallas_call(
-        functools.partial(attend_kernel, min(256, keys)),
-        grid=(heads,),
-        out_shape=(
-            jax.ShapeDtypeStruct((places, features, keys), jnp.bfloat16),
-            jax.ShapeDtypeStruct((heads, length, 1), jnp.float32),
-        ),
-        in_specs=[
-            pl.BlockSpec(memory_space=pltpu.SMEM),
-            pl.BlockSpec((3, places, HEAD_DIM, keys), lambda head: (0, 0, head, 0)),
+        functools.partial(attend_kernel, min(256, keys), chunks, len(shards)),
+        out_shape=[jax.ShapeDtypeStruct(query.shape, jnp.bfloat16)] * 4
+        + [jax.ShapeDtypeStruct((heads, length, 1), jnp.float32)]
+        + [
+            jax.ShapeDtypeStruct((size * shard.shape[0], shard.shape[1]), shard.dtype)
+            for shard in shards
         ],
-        out_specs=(
-            pl.BlockSpec((places, HEAD_DIM, keys), lambda head: (0, head, 0)),
-            pl.BlockSpec((1, length, 1), lambda head: (head, 0, 0)),
-        ),
+        in_specs=[pl.BlockSpec(memory_space=pltpu.SMEM)] + [held] * (3 + len(shards)),
+        out_specs=[held] * 3 + [anywhere, held] + [anywhere] * len(shards),
         scratch_shapes=[
+            pltpu.VMEM(query.shape, jnp.bfloat16),
             pltpu.VMEM((length, HEAD_DIM), jnp.bfloat16),
             pltpu.VMEM((length, HEAD_DIM), jnp.bfloat16),
-        ],
-        compiler_params=pltpu.CompilerParams(vmem_limit_bytes=VMEM_LIMIT),
+        ]
+        + swap_scratch(heads, 3)
+        + swap_scratch(heads, 1)
+        + gather_scratch(shards, chunks),
+        compiler_params=pltpu.CompilerParams(
+            collective_id=collective_id, has_side_effects=True, vmem_limit_bytes=VMEM_LIMIT
+        ),
         name="attend",
-    )(prefix, blocks)
+    )(prefix, query, key, value, *shards)
 
 
 def turn_back(grads, cos_table, sine_table):
@@ -898,97 +1015,129 @@
     )
 
 
-def attend_back_kernel(
-    rows,
-    prefix_ref,
-    blocks_ref,
-    back_ref,
-    log_ref,
-    cos_ref,
-    sine_ref,
-    grads_ref,
-    query_ref,
-    key_ref,
-    attn_ref,
-    key_grad_ref,
-    value_grad_ref,
-):
-    places, keys = blocks_ref.shape[1], blocks_ref.shape[3]
+def attend_back_kernel(rows, chunks, arrays, *refs):
+    prefix_ref, back_in, query_blocks, key_blocks_ref, value_blocks = refs[:5]
+    log_ref, cos_ref, sine_ref = refs[5:8]
+    weight_refs, refs = refs[8 : 8 + arrays], refs[8 + arrays :]
+    landings, reduced_refs, refs = refs[:3], refs[3 : 3 + arrays], refs[3 + arrays :]
+    back_ref, query_out, key_out, value_out = refs[:4]
+    query_ref, key_ref, attn_ref, key_grad_ref, value_grad_ref = refs[4:9]
+    places, features, keys = back_in.shape
+    heads = features // HEAD_DIM
     length = places * keys
     half = HEAD_DIM // 2
     scale = HEAD_DIM ** (-0.5)
+    greet(close_by())
+    begin, landed, sent = swap_steps((back_in,), (back_ref,), *refs[9:12])
+    begin_home, landed_home, sent_home = swap_steps(
+        (query_out, key_out, value_out), landings, *refs[12:15]
+    )
+    stage = reduce_steps(chunks, weight_refs, reduced_refs, refs[15:])
+    for head in range(heads):
+        begin(head)
+    for number in range(len(chunks)):
+        stage(number, 0)
+    acts = [functools.partial(stage, *step) for step in reduce_order(len(chunks), 2)]
+    slots = length // rows
+    planned, left = spaced(acts, slots, heads, 3, 1.2)
     prefix = prefix_ref[0]
-    for block in range(places):
-        span = pl.ds(block * keys, keys)
-        query_ref[span, :] = turn(blocks_ref[0, block] * jnp.bfloat16(scale))
-        key_ref[span, :] = turn(blocks_ref[1, block])
-        attn_ref[span, :] = turn(back_ref[0, block])
-    key_grad_ref[...] = jnp.zeros_like(key_grad_ref)
-    value_grad_ref[...] = jnp.zeros_like(value_grad_ref)
-    for row_block in range(length // rows):
-        span = pl.ds(row_block * rows, rows)
-        home, inside = divmod(row_block * rows, keys)
-        lanes = pl.ds(inside, rows)
-        queries, attn_grad = query_ref[span, :], attn_ref[span, :]
-        queries_low = blocks_ref[0, home, :, lanes] * jnp.bfloat16(scale)
-        attn_low = back_ref[0, home, :, lanes]
-        total = log_ref[0, span, :]
-        reach = key_blocks(row_block, rows, keys, length)
-        weights, pulls = [], []
-        delta = jnp.zeros((rows, 1), jnp.float32)
-        for block in reach:
-            part = dot(queries, blocks_ref[1, block])
-            part = jnp.exp(seen(prefix, row_block, block, rows, keys, part, MASKED) - total)
-            pull = dot(attn_grad, blocks_ref[2, block])
-            delta = delta + jnp.sum(part * pull, axis=1, keepdims=True)
-            weights.append(part)
-            pulls.append(pull)
-        query_grad = jnp.zeros((rows, HEAD_DIM), jnp.float32)
-        for block in reach:
-            key_span = pl.ds(block * keys, keys)
-            score_grad = (weights[block] * (pulls[block] - delta)).astype(jnp.bfloat16)
-            query_grad = query_grad + dot(score_grad, key_ref[key_span, :])
-            key_grad_ref[:, key_span] += dot(queries_low, score_grad)
-            value_grad_ref[:, key_span] += dot(attn_low, weights[block].astype(jnp.bfloat16))
-        low, high = turn_back((query_grad * scale).T, cos_ref[:, span], sine_ref[:, span])
-        grads_ref[0, home, :half, lanes] = low.astype(jnp.bfloat16)
-        grads_ref[0, home, half:, lanes] = high.astype(jnp.bfloat16)
-    for block in range(places):
-        span = pl.ds(block * keys, keys)
-        low, high = turn_back(key_grad_ref[:, span], cos_ref[:, span], sine_ref[:, span])
-        grads_ref[1, block, :half] = low.astype(jnp.bfloat16)
-        grads_ref[1, block, half:] = high.astype(jnp.bfloat16)
-        grads_ref[2, block] = value_grad_ref[:, span].astype(jnp.bfloat16)
-
-
-def attend_back_heads(blocks, back, log_total, prefix, cos_table, sine_table):
-    _, places, features, keys = blocks.shape
+
+    @pl.loop(0, heads)
+    def _(head):
+        landed(head)
+        inside_rows = head_rows(head)
+        for block in range(places):
+            span = pl.ds(block * keys, keys)
+            query_ref[span, :] = turn(query_blocks[block, inside_rows] * jnp.bfloat16(scale))
+            key_ref[span, :] = turn(key_blocks_ref[block, inside_rows])
+            attn_ref[span, :] = turn(back_ref[block, inside_rows])
+        key_grad_ref[...] = jnp.zeros_like(key_grad_ref)
+        value_grad_ref[...] = jnp.zeros_like(value_grad_ref)
+        low_rows = pl.ds(pl.multiple_of(head * HEAD_DIM, half), half)
+        high_rows = pl.ds(pl.multiple_of(head * HEAD_DIM + half, half), half)
+        for row_block in range(length // rows):
+            span = pl.ds(row_block * rows, rows)
+            home, inside = divmod(row_block * rows, keys)
+            lanes = pl.ds(inside, rows)
+            queries, attn_grad = query_ref[span, :], attn_ref[span, :]
+            queries_low = query_blocks[home, inside_rows, lanes] * jnp.bfloat16(scale)
+            attn_low = back_ref[home, inside_rows, lanes]
+            total = log_ref[head, span, :]
+            reach = key_blocks(row_block, rows, keys, length)
+            weights, pulls = [], []
+            delta = jnp.zeros((rows, 1), jnp.float32)
+            for block in reach:
+                part = dot(queries, key_blocks_ref[block, inside_rows])
+                part = jnp.exp(seen(prefix, row_block, block, rows, keys, part, MASKED) - total)
+                pull = dot(attn_grad, value_blocks[block, inside_rows])
+                delta = delta + jnp.sum(part * pull, axis=1, keepdims=True)
+                weights.append(part)
+                pulls.append(pull)
+            query_grad = jnp.zeros((rows, HEAD_DIM), jnp.float32)
+            for block in reach:
+                key_span = pl.ds(block * keys, keys)
+                score_grad = (weights[block] * (pulls[block] - delta)).astype(jnp.bfloat16)
+                query_grad = query_grad + dot(score_grad, key_ref[key_span, :])
+                key_grad_ref[:, key_span] += dot(queries_low, score_grad)
+                value_grad_ref[:, key_span] += dot(attn_low, weights[block].astype(jnp.bfloat16))
+            low, high = turn_back((query_grad * scale).T, cos_ref[:, span], sine_ref[:, span])
+            query_out[home, low_rows, lanes] = low.astype(jnp.bfloat16)
+            query_out[home, high_rows, lanes] = high.astype(jnp.bfloat16)
+            beside(head, row_block, planned)
+        for block in range(places):
+            span = pl.ds(block * keys, keys)
+            low, high = turn_back(key_grad_ref[:, span], cos_ref[:, span], sine_ref[:, span])
+            key_out[block, low_rows] = low.astype(jnp.bfloat16)
+            key_out[block, high_rows] = high.astype(jnp.bfloat16)
+            value_out[block, inside_rows] = value_grad_ref[:, span].astype(jnp.bfloat16)
+        begin_home(head)
+
+    for act in left:
+        act()
+    for head in range(heads):
+        landed_home(head)
+        sent(head)
+        sent_home(head)
+
+
+def attend_back_heads(
+    back, blocks, log_total, prefix, cos_table, sine_table, weight_grads, collective_id
+):
+    places, features, keys = back.shape
     heads = features // HEAD_DIM
     length = places * keys
-    whole = pl.BlockSpec(memory_space=pltpu.VMEM)
+    size = lax.axis_size("fsdp")
+    shapes = [(grad.shape[0] // size, grad.shape[1]) for grad in weight_grads]
+    chunks = column_chunks(shapes, 512)
+    held = pl.BlockSpec(memory_space=pltpu.VMEM)
+    anywhere = pl.BlockSpec(memory_space=pl.ANY)
     return pl.pallas_call(
-        functools.partial(attend_back_kernel, min(256, keys)),
-        grid=(heads,),
-        out_shape=jax.ShapeDtypeStruct(blocks.shape, jnp.bfloat16),
-        in_specs=[
-            pl.BlockSpec(memory_space=pltpu.SMEM),
-            pl.BlockSpec((3, places, HEAD_DIM, keys), lambda head: (0, 0, head, 0)),
-            pl.BlockSpec((1, places, HEAD_DIM, keys), lambda head: (0, 0, head, 0)),
-            pl.BlockSpec((1, length, 1), lambda head: (head, 0, 0)),
-            whole,
-            whole,
-        ],
-        out_specs=pl.BlockSpec((3, places, HEAD_DIM, keys), lambda head: (0, 0, head, 0)),
-        scratch_shapes=[
-            pltpu.VMEM((length, HEAD_DIM), jnp.bfloat16),
-            pltpu.VMEM((length, HEAD_DIM), jnp.bfloat16),
-            pltpu.VMEM((length, HEAD_DIM), jnp.bfloat16),
-            pltpu.VMEM((HEAD_DIM, length), jnp.float32),
-            pltpu.VMEM((HEAD_DIM, length), jnp.float32),
-        ],
-        compiler_params=pltpu.CompilerParams(vmem_limit_bytes=VMEM_LIMIT),
+        functools.partial(attend_back_kernel, min(256, keys), chunks, len(weight_grads)),
+        out_shape=[jax.ShapeDtypeStruct(back.shape, jnp.bfloat16)] * 3
+        + [jax.ShapeDtypeStruct(shape, jnp.bfloat16) for shape in shapes],
+        in_specs=[pl.BlockSpec(memory_space=pltpu.SMEM)]
+        + [held] * 7
+        + [anywhere] * len(weight_grads),
+        out_specs=[anywhere] * 3 + [held] * len(weight_grads),
+        scratch_shapes=[pltpu.VMEM(back.shape, jnp.bfloat16)] * 4
+        + [pltpu.VMEM((length, HEAD_DIM), jnp.bfloat16)] * 3
+        + [pltpu.VMEM((HEAD_DIM, length), jnp.float32)] * 2
+        + swap_scratch(heads, 1)
+        + swap_scratch(heads, 3)
+        + reduce_scratch(chunks, size),
+        compiler_params=pltpu.CompilerParams(
+            collective_id=collective_id, has_side_effects=True, vmem_limit_bytes=VMEM_LIMIT
+        ),
         name="attend_back",
-    )(prefix, blocks, back, log_total, cos_table, sine_table)
+    )(
+        prefix,
+        back,
+        *blocks,
+        log_total,
+        cos_table,
+        sine_table,
+        *[grad.reshape(size, shape[0], shape[1]) for grad, shape in zip(weight_grads, shapes)],
+    )
 
 
 def both_cores(part):
@@ -1059,9 +1208,7 @@
         up_weight.astype(low),
         down_weight.T.astype(low),
     ]
-    gains, full_query, full_key, full_value, full_out, full_gate, full_up, full_down = (
-        gather_shards(shards, 1)
-    )
+    gains, full_query, full_key, full_value, full_out = gather_shards(shards[:5], 1)
     attn_scale = gains_out(gains, 0, quarter).astype(jnp.float32)
     mlp_scale = gains_out(gains, 1, quarter).astype(jnp.float32)
     inputs = jnp.swapaxes(layer_input, 0, 1).astype(jnp.float32)
@@ -1083,11 +1230,15 @@
             )
         return product.astype(low).reshape(blocks_shape)
 
-    blocks = swap_blocks(
-        [project(full_query, True), project(full_key, True), project(full_value, False)], 2
-    )
-    mixed_heads, log_total = attend(blocks, prefix)
-    mixed_low = swap_blocks([mixed_heads], 3).reshape(seq_count, local, block_len)
+    *blocks, mixed_low, log_total, full_gate, full_up, full_down = attend(
+        project(full_query, True),
+        project(full_key, True),
+        project(full_value, False),
+        shards[5:],
+        prefix,
+        2,
+    )
+    mixed_low = mixed_low.reshape(seq_count, local, block_len)
     hidden = inputs + both_cores(matmul("bes,de->bsd", mixed_low, full_out))
     hnorm_low = norm_rows(hidden, mlp_scale).astype(low)
     gate_out = matmul("bsd,df->bsf", hnorm_low, full_gate)
@@ -1112,11 +1263,18 @@
     hidden_grad = cotangent.astype(jnp.float32) + hidden_back
     hidden_low = hidden_grad.astype(low)
     attn_grad = matmul("bsd,de->bes", hidden_low, full_out).astype(low)
-    back = swap_blocks([attn_grad.reshape(blocks_shape)], 4)
     out_w_grad = matmul("bsd,bes->de", hidden_low, mixed_low)
-    grads = attend_back_heads(blocks, back, log_total, prefix, cos_table, sine_table)
-    grads = swap_blocks([grads[0], grads[1], grads[2]], 5)
-    grads = grads.reshape(3, seq_count, local, block_len)
+    *grads, down, gate, up, out = attend_back_heads(
+        attn_grad.reshape(blocks_shape),
+        blocks,
+        log_total,
+        prefix,
+        cos_table,
+        sine_table,
+        [grad.astype(low) for grad in (down_w_grad, gate_w_grad, up_w_grad, out_w_grad)],
+        3,
+    )
+    grads = [grad.reshape(seq_count, local, block_len) for grad in grads]
     normed_part = (
         matmul("bes,de->bsd", grads[0], full_query)
         + matmul("bes,de->bsd", grads[1], full_key)
@@ -1126,10 +1284,6 @@
     input_back, attn_gain_part = norm_back(inputs, attn_scale, normed_grad)
     input_grad = (hidden_grad + input_back).astype(low)
     weight_grads = [
-        down_w_grad,
-        gate_w_grad,
-        up_w_grad,
-        out_w_grad,
         matmul("bsd,bes->de", normed_low, grads[0]),
         matmul("bsd,bes->de", normed_low, grads[1]),
         matmul("bsd,bes->de", normed_low, grads[2]),
@@ -1138,9 +1292,9 @@
     gain_parts = jax.vmap(gains_in)(
         attn_gain_part.reshape(count, -1), mlp_gain_part.reshape(count, -1)
     ).reshape(-1, 128)
-    reduced = reduce_grads([gain_parts] + [grad.astype(low) for grad in weight_grads], 6)
-    gains, down, gate, up, out, query, key, value = [
-        total.astype(jnp.float32) for total in reduced
+    reduced = reduce_grads([gain_parts] + [grad.astype(low) for grad in weight_grads], 4)
+    gains, query, key, value, down, gate, up, out = [
+        total.astype(jnp.float32) for total in (*reduced, down, gate, up, out)
     ]
     return (
         jnp.swapaxes(layer_output, 0, 1),

time: 402 us -> 343 us (0.85)
  Pallas kernels: 289 us -> 234 us
  local copies, waits for them, and re-layouts: 18.4 us -> 13.7 us
    pallas_call x1, Pallas kernels: 97.5 us -> 36.1 us  [reduce_grads(): pl.pallas_call(functools.partial(reduce_kernel, chunks, len(grads)), out_...]
    pallas_call x6 -> x2, Pallas kernels: 134 us -> 169 us  [the longest x1 104 us: attend_back_heads(): pl.pallas_call(functools.partial(attend_back_kernel, min(256, keys), chun...]
    pallas_call x1, Pallas kernels: 57.9 us -> 29.5 us  [gather_shards(): pl.pallas_call(functools.partial(gather_kernel, chunks, len(shards)), out...]
    unnamed x70 -> x62, local copies, waits for them, and re-layouts: 9 us -> 8.5 us
  transfers between devices with their start and end apart: 4 -> 4, of which waited for: 0 -> 0; matrix products, arithmetic and copies ran while one was open for 7% -> 9% of each run, Pallas kernels for 0% -> 0%
where the time goes in v2:
time: 343 us; the launch traced here: 337 us
  Pallas kernels  234 us (68%)
  matrix products  48.5 us (14%)
  other arithmetic  38.1 us (11%)
  local copies, waits for them, and re-layouts  13.7 us (4%)
    pallas_call x1, Pallas kernels, attend_back_heads(): pl.pallas_call(functools.partial(attend_back_kernel, min(256, keys), chun...  104 us
    pallas_call x1, Pallas kernels, attend(): pl.pallas_call(functools.partial(attend_kernel, min(256, keys), chunks, l...  65.1 us
    dot_general x21, matrix products, matmul(): return jnp.einsum(spec, left, right, preferred_element_type=jnp.float32)  48.5 us
    pallas_call x1, Pallas kernels, reduce_grads(): pl.pallas_call(functools.partial(reduce_kernel, chunks, len(grads)), out_...  36.1 us
    pallas_call x1, Pallas kernels, gather_shards(): pl.pallas_call(functools.partial(gather_kernel, chunks, len(shards)), out...  29.5 us
    unnamed x62, local copies, waits for them, and re-layouts  8.5 us
  transfers between devices with their start and end apart: 4, of which 0 were waited for; matrix products, arithmetic and copies ran while one was open for 9% of the time, Pallas kernels for 0%

profile of v2, /device:TPU:0, one launch (start us, length us, event | category | flops | bytes accessed | tf_op | source)
XLA Modules:
  0.0 336.9 jit_solution(6742924555797832703)
XLA Ops:
  2.4 1.9 fusion.4
  4.3 1.7 convert_element_type.191.refs_1_
  8.9 0.8 convert_element_type.204.refs_5_
  10.6 1.8 fusion.50
  13.0 29.5 %gather_shards.1 = (bf16[256,128]{1,0:T(8,128)(2,1)}, bf16[768,384]{1,0:T(8,128)(2,1)}, bf16[768,384]{1,0:T(8,128)(2,1)}, bf16[768,384]{1,0:T(8,128)(2,1)}, bf16[768,384]{1,0:T(8,128)(2,1)}) custom-call(bf16[64,128]{1,0:T(8,128)(2,1)} %bitcast.200, bf16[192,384]{1,0:T(8,128)(2,1)} %convert_element_type.191.refs_1_, ...), custom_call_target="tpu_custom_call" | custom-call | tf_op jit(solution)/shard_map/gather_shards/pallas_call | solution.py:604
  42.5 0.9 fusion.51
  43.4 3.0 convolution_convert_fusion.3
  46.4 1.0 fusion.43
  47.5 2.1 fusion.47
  50.2 0.8 constant_dynamic-slice_fusion
  51.1 1.9 subtract_convert_fusion
  53.0 1.0 pad_maximum_fusion.1
  53.9 0.9 pad_maximum_fusion
  54.9 65.1 %attend.1 = (bf16[4,192,512]{2,1,0:T(8,128)(2,1)}, bf16[4,192,512]{2,1,0:T(8,128)(2,1)}, bf16[4,192,512]{2,1,0:T(8,128)(2,1)}, bf16[4,192,512]{2,1,0:T(8,128)(2,...) custom-call(s32[1]{0:T(128)} %dynamic_slice.9.refs_0_, ...), custom_call_target="tpu_custom_call" | custom-call | tf_op jit(solution)/shard_map/attend/pallas_call | solution.py:984
  120.0 2.3 convolution_convert_fusion
  122.4 3.8 %fusion.18 = f32[1024,2,512]{0,2,1:T(8,128)S(1)} fusion(bf16[768,1024]{1,0:T(8,128)(2,1)} %get-tuple-element.43, bf16[512,2,768]{2,1,0:T(2,128)(2,1)} %param.13), kind=kOutput, calls=%fused_computation.43 | convolution fusion | flops 1610612736 | bytes 7340032 | tf_op jit(solution)/shard_map/bsd,df->bsf/dot_general | solution.py:1151
  126.2 2.1 multiply_reduce_fusion.2
  128.7 1.1 copy-done.26
  129.7 1.8 fusion.23
  131.6 4.4 %fusion.2 = (bf16[2,512,1024]{2,1,0:T(8,128)(2,1)S(1)}, bf16[2,512,1024]{2,1,0:T(8,128)(2,1)S(1)}, bf16[2,512,1024]{2,1,0:T(8,128)(2,1)S(1)}) fusion(f32[1024,2,512]{0,2,1:T(8,128)S(1)} %fusion.18, f32[2,512,1024]{2,1,0:T(8,128)S(1)} %fusion.23, bf16[2,512,768]{2,1,0:T(8,128)(2,1)S(1)} %multiply_convert_fusion.1, bf16[768,1024]{1,0:T(8,128)(2,1)S(1)} %copy-done.27), kind=kOutput, calls=%fused_computation.4 | convolution fusion | flops 1626341376 | bytes 17825792 | tf_op jit(solution)/shard_map/bsd,df->bsf/dot_general | solution.py:1151
  136.0 1.8 fusion.25
  137.8 1.9 add_convert_fusion.1
  140.3 1.8 convolution_convert_fusion.1
  142.2 3.1 bitcast_convert_fusion
  145.2 3.0 bitcast_convert_fusion.1
  148.3 3.0 bitcast_convert_fusion.2
  151.3 1.7 multiply_reduce_fusion
  153.1 2.4 subtract_add_fusion
  155.5 1.8 fusion.29
  157.4 1.7 convolution_convert_fusion.2
  159.1 103.8 %attend_back.1 = (bf16[4,192,512]{2,1,0:T(8,128)(2,1)}, bf16[4,192,512]{2,1,0:T(8,128)(2,1)}, bf16[4,192,512]{2,1,0:T(8,128)(2,1)}, bf16[192,1024]{1,0:T(8,128)(...) custom-call(s32[1]{0:T(128)} %dynamic_slice.9.refs_0_, ...), custom_call_target="tpu_custom_call" | custom-call | tf_op jit(solution)/shard_map/attend_back/pallas_call | solution.py:1114
  262.9 2.4 fusion.45
  265.4 1.0 fusion.41
  266.7 2.2 add_convert_fusion
  269.7 4.2 %copy.65 = bf16[512,2,768]{2,1,0:T(2,128)(2,1)} copy(bf16[512,2,768]{2,0,1:T(8,128)(2,1)} %get-tuple-element.95) | data formatting | bytes 3145728
  274.0 1.0 convert_element_type.243
  274.9 1.0 convert_element_type.244
  276.6 1.0 convert_bitcast_fusion
  277.6 2.1 fusion.31
  279.7 2.1 fusion.30
  281.8 2.1 fusion.32
  283.9 3.4 %fusion.12 = (bf16[768]{0:T(1024)(128)(2,1)S(1)}, f32[2,512]{1,0:T(2,128)S(1)}) fusion(bf16[2,512,768]{2,1,0:T(8,128)(2,1)} %collective-permute-done.3, bf16[2,512,768]{2,1,0:T(8,128)(2,1)} %add_convert_fusion, f32[2,512]{1,0:T(2,128)S(1)} %add_rsqrt_fusion.1, bf16[512,2,768]{2,1,0:T(2,128)(2,1)S(1)} %copy-done.1, f32[768]{0:T(1024)S(1)} %reshape.167), kind=kLoop, calls=%fused_computation.25 | loop fusion | flops 7862528 | bytes 4731392 | tf_op jit(solution)/shard_map/reduce_sum | solution.py:1165
  287.3 2.7 fusion.16
  290.0 2.8 copy.66
  293.6 36.1 %reduce_grads.1 = (bf16[64,128]{1,0:T(8,128)(2,1)}, bf16[192,384]{1,0:T(8,128)(2,1)}, bf16[192,384]{1,0:T(8,128)(2,1)}, bf16[192,384]{1,0:T(8,128)(2,1)}) custom-call(bf16[4,64,128]{2,1,0:T(8,128)(2,1)} %bitcast.199, bf16[4,192,384]{2,1,0:T(8,128)(2,1)} %bitcast.197, bf16[4,192,384]{2,1,0:T(8,128)(2,1)} %bitcast.196, bf16[4,192,384]{2,1,0:T(8,128)(2,1)} %bitcast.198), custom_call_target="tpu_custom_call" | custom-call | tf_op jit(solution)/shard_map/reduce_grads/pallas_call | solution.py:782
  331.7 1.6 convert_element_type.240
  333.4 1.6 convert_element_type.241
  335.0 1.6 convert_element_type.242
  (96 shorter events, 12.6 us)
Async XLA Ops:
  0.6 5.4 %copy-start.21 = (f32[192,384]{1,0:T(8,128)S(1)}, f32[192,384]{1,0:T(8,128)}, u32[]{:S(2)}) copy-start(f32[192,384]{1,0:T(8,128)} %param.18) | copy-start | bytes 884740
  0.7 6.0 %copy-start.22 = (f32[192,384]{1,0:T(8,128)S(1)}, f32[192,384]{1,0:T(8,128)}, u32[]{:S(2)}) copy-start(f32[192,384]{1,0:T(8,128)} %param.19) | copy-start | bytes 884740
  0.7 6.7 %copy-start.23 = (f32[384,192]{0,1:T(8,128)S(1)}, f32[384,192]{0,1:T(8,128)}, u32[]{:S(2)}) copy-start(f32[384,192]{0,1:T(8,128)} %param.20) | copy-start | bytes 884740
  0.7 7.4 %copy-start.6 = (f32[192,1024]{1,0:T(8,128)S(1)}, f32[192,1024]{1,0:T(8,128)}, u32[]{:S(2)}) copy-start(f32[192,1024]{1,0:T(8,128)} %param.21) | copy-start | bytes 2359300
  2.4 6.5 %copy-start.7 = (f32[192,1024]{1,0:T(8,128)S(1)}, f32[192,1024]{1,0:T(8,128)}, u32[]{:S(2)}) copy-start(f32[192,1024]{1,0:T(8,128)} %param.22) | copy-start | bytes 2359300
  4.3 5.4 %copy-start.8 = (f32[1024,192]{0,1:T(8,128)S(1)}, f32[1024,192]{0,1:T(8,128)}, u32[]{:S(2)}) copy-start(f32[1024,192]{0,1:T(8,128)} %param.23) | copy-start | bytes 2359300
  8.1 35.4 %copy-start = (bf16[512,2,768]{2,1,0:T(2,128)(2,1)S(1)}, bf16[512,2,768]{2,1,0:T(2,128)(2,1)}, u32[]{:S(2)}) copy-start(bf16[512,2,768]{2,1,0:T(2,128)(2,1)} %param.12) | copy-start | bytes 4718596
  12.3 37.9 %copy-start.3 = (f32[32,2048]{1,0:T(8,128)}, f32[32,2048]{1,0:T(8,128)S(1)}, u32[]{:S(2)}) copy-start(f32[32,2048]{1,0:T(8,128)S(1)} %get-tuple-element.102.refs_6_) | copy-start | bytes 786436
  43.4 3.0 copy-start.14
  46.4 1.1 copy-start.16
  47.5 2.2 copy-start.28
  122.3 3.9 %collective-permute-start = (bf16[2,512,768]{2,1,0:T(8,128)(2,1)S(1)}, bf16[2,512,768]{2,1,0:T(8,128)(2,1)}, u32[]{:S(2)}, u32[]{:S(2)}) collective-permute-start(bf16[2,512,768]{2,1,0:T(8,128)(2,1)S(1)} %convolution_convert_fusion), channel_id=1, source_target_pairs={{0,1},{1,0},{2,3},{3,2},{4,5},{5,4},{6,7},{7,6},{8,9},{9,8},{10,11... | collective-permute-start | bytes 4718600 | tf_op jit(solution)/shard_map/ppermute | solution.py:1146
  128.3 1.4 copy-start.26
  129.7 1.8 copy-start.27
  137.8 2.5 copy-start.25
  139.7 11.6 %collective-permute-start.2 = (bf16[2,512,768]{2,1,0:T(8,128)(2,1)S(1)}, bf16[2,512,768]{2,1,0:T(8,128)(2,1)S(1)}, u32[]{:S(2)}, u32[]{:S(2)}) collective-permute-start(bf16[2,512,768]{2,1,0:T(8,128)(2,1)S(1)} %add_convert_fusion.1), channel_id=1, source_target_pairs={{0,1},{1,0},{2,3},{3,2},{4,5},{5,4},{6,7},{7,6},{8,9},{9,8},{10,11... | collective-permute-start | bytes 4718600 | tf_op jit(solution)/shard_map/ppermute | solution.py:1146
  142.1 11.0 %collective-permute-start.1 = (bf16[2,512,768]{2,1,0:T(8,128)(2,1)S(1)}, bf16[2,512,768]{2,1,0:T(8,128)(2,1)S(1)}, u32[]{:S(2)}, u32[]{:S(2)}) collective-permute-start(bf16[2,512,768]{2,1,0:T(8,128)(2,1)S(1)} %convolution_convert_fusion.1), channel_id=1, source_target_pairs={{0,1},{1,0},{2,3},{3,2},{4,5},{5,4},{6,7},{7,6},{8,9},{9,8},{10,11... | collective-permute-start | bytes 4718600 | tf_op jit(solution)/shard_map/ppermute | solution.py:1146
  145.2 3.0 copy-start.2
  153.0 2.5 copy-start.9
  155.5 1.9 copy-start.17
  262.9 2.4 copy-start.11
  262.9 2.4 copy-start.15
  265.4 1.1 copy-start.4
  265.4 1.3 copy-start.13
  268.9 5.1 %copy-start.20 = (bf16[192,1024]{1,0:T(8,128)(2,1)S(1)}, bf16[192,1024]{1,0:T(8,128)(2,1)}, u32[]{:S(2)}) copy-start(bf16[192,1024]{1,0:T(8,128)(2,1)} %get-tuple-element.56) | copy-start | bytes 1179652
  268.9 15.0 %collective-permute-start.3 = (bf16[2,512,768]{2,1,0:T(8,128)(2,1)}, bf16[2,512,768]{2,1,0:T(8,128)(2,1)}, u32[]{:S(2)}, u32[]{:S(2)}) collective-permute-start(bf16[2,512,768]{2,1,0:T(8,128)(2,1)} %add_convert_fusion), channel_id=1, source_target_pairs={{0,1},{1,0},{2,3},{3,2},{4,5},{5,4},{6,7},{7,6},{8,9},{9,8},{10,11... | collective-permute-start | bytes 4718600 | tf_op jit(solution)/shard_map/ppermute | solution.py:1146
  269.7 5.2 %copy-start.19 = (bf16[192,1024]{1,0:T(8,128)(2,1)S(1)}, bf16[192,1024]{1,0:T(8,128)(2,1)}, u32[]{:S(2)}) copy-start(bf16[192,1024]{1,0:T(8,128)(2,1)} %get-tuple-element.57) | copy-start | bytes 1179652
  269.7 6.2 %copy-start.24 = (bf16[192,384]{1,0:T(8,128)(2,1)S(1)}, bf16[192,384]{1,0:T(8,128)(2,1)}, u32[]{:S(2)}) copy-start(bf16[192,384]{1,0:T(8,128)(2,1)} %get-tuple-element.55) | copy-start | bytes 442372
  273.9 2.7 copy-start.18
  273.9 3.6 %copy-start.1 = (bf16[512,2,768]{2,1,0:T(2,128)(2,1)S(1)}, bf16[512,2,768]{2,1,0:T(2,128)(2,1)}, u32[]{:S(2)}) copy-start(bf16[512,2,768]{2,1,0:T(2,128)(2,1)} %param.12) | copy-start | bytes 4718596
  273.9 3.6 %copy-start.12 = (bf16[4,192,512]{2,1,0:T(8,128)(2,1)S(1)}, bf16[4,192,512]{2,1,0:T(8,128)(2,1)}, u32[]{:S(2)}) copy-start(bf16[4,192,512]{2,1,0:T(8,128)(2,1)} %get-tuple-element.49) | copy-start | bytes 2359300
  277.6 2.1 copy-start.10
  279.7 2.1 copy-start.5

commit v3 on v2

--- a/solution.py
+++ b/solution.py
@@ -598,7 +598,7 @@
 
 
 def gather_shards(shards, collective_id):
-    chunks = column_chunks([shard.shape for shard in shards], 512)
+    chunks = column_chunks([shard.shape for shard in shards], 128)
     size = lax.axis_size("fsdp")
     anywhere = pl.BlockSpec(memory_space=pl.ANY)
     return pl.pallas_call(
@@ -777,7 +777,7 @@
 def reduce_grads(grads, collective_id):
     size = lax.axis_size("fsdp")
     shapes = [(grad.shape[0] // size, grad.shape[1]) for grad in grads]
-    chunks = column_chunks(shapes, 512)
+    chunks = column_chunks(shapes, 128)
     anywhere = pl.BlockSpec(memory_space=pl.ANY)
     return pl.pallas_call(
         functools.partial(reduce_kernel, chunks, len(grads)),

time: 343 us -> 353 us (1.029)
  Pallas kernels: 234 us -> 244 us
    pallas_call x1, Pallas kernels: 36.1 us -> 42.9 us  [reduce_grads(): pl.pallas_call(functools.partial(reduce_kernel, chunks, len(grads)), out_...]
where the time goes in v3:
time: 353 us; the launch traced here: 346 us
  Pallas kernels  244 us (69%)
  matrix products  48.5 us (14%)
  other arithmetic  38.1 us (11%)
  local copies, waits for them, and re-layouts  13.7 us (4%)
    pallas_call x1, Pallas kernels, attend_back_heads(): pl.pallas_call(functools.partial(attend_back_kernel, min(256, keys), chun...  104 us
    pallas_call x1, Pallas kernels, attend(): pl.pallas_call(functools.partial(attend_kernel, min(256, keys), chunks, l...  65.2 us
    dot_general x21, matrix products, matmul(): return jnp.einsum(spec, left, right, preferred_element_type=jnp.float32)  48.5 us
    pallas_call x1, Pallas kernels, reduce_grads(): pl.pallas_call(functools.partial(reduce_kernel, chunks, len(grads)), out_...  42.9 us
    pallas_call x1, Pallas kernels, gather_shards(): pl.pallas_call(functools.partial(gather_kernel, chunks, len(shards)), out...  31.7 us
    unnamed x62, local copies, waits for them, and re-layouts  8.5 us
  transfers between devices with their start and end apart: 4, of which 0 were waited for; matrix products, arithmetic and copies ran while one was open for 9% of the time, Pallas kernels for 0%

profile of v3, /device:TPU:0, one launch (start us, length us, event | category | flops | bytes accessed | tf_op | source)
XLA Modules:
  0.0 345.9 jit_solution(10581170429764733773)
XLA Ops:
  2.4 1.9 fusion.4
  4.3 1.7 convert_element_type.191.refs_1_
  8.9 0.8 convert_element_type.204.refs_5_
  10.6 1.8 fusion.50
  13.0 31.7 %gather_shards.1 = (bf16[256,128]{1,0:T(8,128)(2,1)}, bf16[768,384]{1,0:T(8,128)(2,1)}, bf16[768,384]{1,0:T(8,128)(2,1)}, bf16[768,384]{1,0:T(8,128)(2,1)}, bf16[768,384]{1,0:T(8,128)(2,1)}) custom-call(bf16[64,128]{1,0:T(8,128)(2,1)} %bitcast.200, bf16[192,384]{1,0:T(8,128)(2,1)} %convert_element_type.191.refs_1_, ...), custom_call_target="tpu_custom_call" | custom-call | tf_op jit(solution)/shard_map/gather_shards/pallas_call | solution.py:604
  44.6 0.9 fusion.51
  45.6 3.0 convolution_convert_fusion.3
  48.6 1.0 fusion.43
  49.7 2.1 fusion.47
  52.4 0.8 constant_dynamic-slice_fusion
  53.3 1.9 subtract_convert_fusion
  55.1 1.0 pad_maximum_fusion.1
  56.1 0.9 pad_maximum_fusion
  57.0 65.2 %attend.1 = (bf16[4,192,512]{2,1,0:T(8,128)(2,1)}, bf16[4,192,512]{2,1,0:T(8,128)(2,1)}, bf16[4,192,512]{2,1,0:T(8,128)(2,1)}, bf16[4,192,512]{2,1,0:T(8,128)(2,...) custom-call(s32[1]{0:T(128)} %dynamic_slice.9.refs_0_, ...), custom_call_target="tpu_custom_call" | custom-call | tf_op jit(solution)/shard_map/attend/pallas_call | solution.py:984
  122.2 2.3 convolution_convert_fusion
  124.7 3.8 %fusion.18 = f32[1024,2,512]{0,2,1:T(8,128)S(1)} fusion(bf16[768,1024]{1,0:T(8,128)(2,1)} %get-tuple-element.43, bf16[512,2,768]{2,1,0:T(2,128)(2,1)} %param.13), kind=kOutput, calls=%fused_computation.43 | convolution fusion | flops 1610612736 | bytes 7340032 | tf_op jit(solution)/shard_map/bsd,df->bsf/dot_general | solution.py:1151
  128.5 2.1 multiply_reduce_fusion.2
  130.9 1.1 copy-done.26
  132.0 1.8 fusion.23
  133.8 4.4 %fusion.2 = (bf16[2,512,1024]{2,1,0:T(8,128)(2,1)S(1)}, bf16[2,512,1024]{2,1,0:T(8,128)(2,1)S(1)}, bf16[2,512,1024]{2,1,0:T(8,128)(2,1)S(1)}) fusion(f32[1024,2,512]{0,2,1:T(8,128)S(1)} %fusion.18, f32[2,512,1024]{2,1,0:T(8,128)S(1)} %fusion.23, bf16[2,512,768]{2,1,0:T(8,128)(2,1)S(1)} %multiply_convert_fusion.1, bf16[768,1024]{1,0:T(8,128)(2,1)S(1)} %copy-done.27), kind=kOutput, calls=%fused_computation.4 | convolution fusion | flops 1626341376 | bytes 17825792 | tf_op jit(solution)/shard_map/bsd,df->bsf/dot_general | solution.py:1151
  138.2 1.8 fusion.25
  140.1 1.9 add_convert_fusion.1
  142.5 1.8 convolution_convert_fusion.1
  144.4 3.1 bitcast_convert_fusion
  147.5 3.0 bitcast_convert_fusion.1
  150.5 3.0 bitcast_convert_fusion.2
  153.5 1.7 multiply_reduce_fusion
  155.3 2.4 subtract_add_fusion
  157.8 1.8 fusion.29
  159.6 1.7 convolution_convert_fusion.2
  161.4 103.8 %attend_back.1 = (bf16[4,192,512]{2,1,0:T(8,128)(2,1)}, bf16[4,192,512]{2,1,0:T(8,128)(2,1)}, bf16[4,192,512]{2,1,0:T(8,128)(2,1)}, bf16[192,1024]{1,0:T(8,128)(...) custom-call(s32[1]{0:T(128)} %dynamic_slice.9.refs_0_, ...), custom_call_target="tpu_custom_call" | custom-call | tf_op jit(solution)/shard_map/attend_back/pallas_call | solution.py:1114
  265.2 2.4 fusion.45
  267.7 1.0 fusion.41
  268.9 2.2 add_convert_fusion
  272.0 4.2 %copy.65 = bf16[512,2,768]{2,1,0:T(2,128)(2,1)} copy(bf16[512,2,768]{2,0,1:T(8,128)(2,1)} %get-tuple-element.95) | data formatting | bytes 3145728
  276.2 1.0 convert_element_type.243
  277.2 1.0 convert_element_type.244
  278.9 1.0 convert_bitcast_fusion
  279.8 2.1 fusion.31
  282.0 2.1 fusion.30
  284.1 2.1 fusion.32
  286.2 3.4 fusion.12
  289.6 2.7 fusion.16
  292.3 2.8 copy.66
  295.8 42.9 %reduce_grads.1 = (bf16[64,128]{1,0:T(8,128)(2,1)}, bf16[192,384]{1,0:T(8,128)(2,1)}, bf16[192,384]{1,0:T(8,128)(2,1)}, bf16[192,384]{1,0:T(8,128)(2,1)}) custom-call(bf16[4,64,128]{2,1,0:T(8,128)(2,1)} %bitcast.199, bf16[4,192,384]{2,1,0:T(8,128)(2,1)} %bitcast.197, bf16[4,192,384]{2,1,0:T(8,128)(2,1)} %bitcast.196, bf16[4,192,384]{2,1,0:T(8,128)(2,1)} %bitcast.198), custom_call_target="tpu_custom_call" | custom-call | tf_op jit(solution)/shard_map/reduce_grads/pallas_call | solution.py:782
  340.7 1.6 convert_element_type.240
  342.4 1.6 convert_element_type.241
  344.0 1.6 convert_element_type.242
  (96 shorter events, 12.6 us)
Async XLA Ops:
  0.6 5.4 %copy-start.21 = (f32[192,384]{1,0:T(8,128)S(1)}, f32[192,384]{1,0:T(8,128)}, u32[]{:S(2)}) copy-start(f32[192,384]{1,0:T(8,128)} %param.18) | copy-start | bytes 884740
  0.7 6.0 %copy-start.22 = (f32[192,384]{1,0:T(8,128)S(1)}, f32[192,384]{1,0:T(8,128)}, u32[]{:S(2)}) copy-start(f32[192,384]{1,0:T(8,128)} %param.19) | copy-start | bytes 884740
  0.7 6.7 %copy-start.23 = (f32[384,192]{0,1:T(8,128)S(1)}, f32[384,192]{0,1:T(8,128)}, u32[]{:S(2)}) copy-start(f32[384,192]{0,1:T(8,128)} %param.20) | copy-start | bytes 884740
  0.7 7.4 %copy-start.6 = (f32[192,1024]{1,0:T(8,128)S(1)}, f32[192,1024]{1,0:T(8,128)}, u32[]{:S(2)}) copy-start(f32[192,1024]{1,0:T(8,128)} %param.21) | copy-start | bytes 2359300
  2.4 6.5 %copy-start.7 = (f32[192,1024]{1,0:T(8,128)S(1)}, f32[192,1024]{1,0:T(8,128)}, u32[]{:S(2)}) copy-start(f32[192,1024]{1,0:T(8,128)} %param.22) | copy-start | bytes 2359300
  4.3 5.4 %copy-start.8 = (f32[1024,192]{0,1:T(8,128)S(1)}, f32[1024,192]{0,1:T(8,128)}, u32[]{:S(2)}) copy-start(f32[1024,192]{0,1:T(8,128)} %param.23) | copy-start | bytes 2359300
  8.1 37.6 %copy-start = (bf16[512,2,768]{2,1,0:T(2,128)(2,1)S(1)}, bf16[512,2,768]{2,1,0:T(2,128)(2,1)}, u32[]{:S(2)}) copy-start(bf16[512,2,768]{2,1,0:T(2,128)(2,1)} %param.12) | copy-start | bytes 4718596
  12.3 40.1 %copy-start.3 = (f32[32,2048]{1,0:T(8,128)}, f32[32,2048]{1,0:T(8,128)S(1)}, u32[]{:S(2)}) copy-start(f32[32,2048]{1,0:T(8,128)S(1)} %get-tuple-element.102.refs_6_) | copy-start | bytes 786436
  45.6 3.0 copy-start.14
  48.6 1.1 copy-start.16
  49.7 2.2 copy-start.28
  124.5 3.9 %collective-permute-start = (bf16[2,512,768]{2,1,0:T(8,128)(2,1)S(1)}, bf16[2,512,768]{2,1,0:T(8,128)(2,1)}, u32[]{:S(2)}, u32[]{:S(2)}) collective-permute-start(bf16[2,512,768]{2,1,0:T(8,128)(2,1)S(1)} %convolution_convert_fusion), channel_id=1, source_target_pairs={{0,1},{1,0},{2,3},{3,2},{4,5},{5,4},{6,7},{7,6},{8,9},{9,8},{10,11... | collective-permute-start | bytes 4718600 | tf_op jit(solution)/shard_map/ppermute | solution.py:1146
  130.6 1.4 copy-start.26
  132.0 1.8 copy-start.27
  140.0 2.5 copy-start.25
  141.9 11.6 %collective-permute-start.2 = (bf16[2,512,768]{2,1,0:T(8,128)(2,1)S(1)}, bf16[2,512,768]{2,1,0:T(8,128)(2,1)S(1)}, u32[]{:S(2)}, u32[]{:S(2)}) collective-permute-start(bf16[2,512,768]{2,1,0:T(8,128)(2,1)S(1)} %add_convert_fusion.1), channel_id=1, source_target_pairs={{0,1},{1,0},{2,3},{3,2},{4,5},{5,4},{6,7},{7,6},{8,9},{9,8},{10,11... | collective-permute-start | bytes 4718600 | tf_op jit(solution)/shard_map/ppermute | solution.py:1146
  144.3 11.0 %collective-permute-start.1 = (bf16[2,512,768]{2,1,0:T(8,128)(2,1)S(1)}, bf16[2,512,768]{2,1,0:T(8,128)(2,1)S(1)}, u32[]{:S(2)}, u32[]{:S(2)}) collective-permute-start(bf16[2,512,768]{2,1,0:T(8,128)(2,1)S(1)} %convolution_convert_fusion.1), channel_id=1, source_target_pairs={{0,1},{1,0},{2,3},{3,2},{4,5},{5,4},{6,7},{7,6},{8,9},{9,8},{10,11... | collective-permute-start | bytes 4718600 | tf_op jit(solution)/shard_map/ppermute | solution.py:1146
  147.5 3.0 copy-start.2
  155.3 2.5 copy-start.9
  157.8 1.9 copy-start.17
  265.2 2.4 copy-start.11
  265.2 2.4 copy-start.15
  267.6 1.1 copy-start.4
  267.7 1.3 copy-start.13
  271.1 5.1 %copy-start.20 = (bf16[192,1024]{1,0:T(8,128)(2,1)S(1)}, bf16[192,1024]{1,0:T(8,128)(2,1)}, u32[]{:S(2)}) copy-start(bf16[192,1024]{1,0:T(8,128)(2,1)} %get-tuple-element.56) | copy-start | bytes 1179652
  271.1 15.0 %collective-permute-start.3 = (bf16[2,512,768]{2,1,0:T(8,128)(2,1)}, bf16[2,512,768]{2,1,0:T(8,128)(2,1)}, u32[]{:S(2)}, u32[]{:S(2)}) collective-permute-start(bf16[2,512,768]{2,1,0:T(8,128)(2,1)} %add_convert_fusion), channel_id=1, source_target_pairs={{0,1},{1,0},{2,3},{3,2},{4,5},{5,4},{6,7},{7,6},{8,9},{9,8},{10,11... | collective-permute-start | bytes 4718600 | tf_op jit(solution)/shard_map/ppermute | solution.py:1146
  272.0 5.2 %copy-start.19 = (bf16[192,1024]{1,0:T(8,128)(2,1)S(1)}, bf16[192,1024]{1,0:T(8,128)(2,1)}, u32[]{:S(2)}) copy-start(bf16[192,1024]{1,0:T(8,128)(2,1)} %get-tuple-element.57) | copy-start | bytes 1179652
  272.0 6.2 %copy-start.24 = (bf16[192,384]{1,0:T(8,128)(2,1)S(1)}, bf16[192,384]{1,0:T(8,128)(2,1)}, u32[]{:S(2)}) copy-start(bf16[192,384]{1,0:T(8,128)(2,1)} %get-tuple-element.55) | copy-start | bytes 442372
  276.2 2.7 copy-start.18
  276.2 3.6 %copy-start.1 = (bf16[512,2,768]{2,1,0:T(2,128)(2,1)S(1)}, bf16[512,2,768]{2,1,0:T(2,128)(2,1)}, u32[]{:S(2)}) copy-start(bf16[512,2,768]{2,1,0:T(2,128)(2,1)} %param.12) | copy-start | bytes 4718596
  276.2 3.6 %copy-start.12 = (bf16[4,192,512]{2,1,0:T(8,128)(2,1)S(1)}, bf16[4,192,512]{2,1,0:T(8,128)(2,1)}, u32[]{:S(2)}) copy-start(bf16[4,192,512]{2,1,0:T(8,128)(2,1)} %get-tuple-element.49) | copy-start | bytes 2359300
  279.8 2.1 copy-start.10
  282.0 2.1 copy-start.5
